TPU v7x, 32 devices: a 4x4x1 block of a 4x4x8 slice. The times are simulated.
32 devices in a mesh: batch: 1 (over z), w: 4 (over y), h: 8 (over x, core).
Axes of the slice: x: 4, y: 4, z: 1, core: 2. Of those that a mesh axis runs over, the one named last changes fastest.
The devices are a block of a 4x4x8 slice.
Arguments:
- image: bfloat16 [512, 128, 256, 4], P('batch', 'h', 'w')
- down_w1: bfloat16 [3, 3, 4, 32], replicated
- down_v1: float32 [3, 32], replicated
- refine_w1: bfloat16 [3, 3, 32, 32], replicated
- refine_v1: float32 [3, 32], replicated
- down_w2: bfloat16 [3, 3, 32, 64], replicated
- down_v2: float32 [3, 64], replicated
- refine_w2: bfloat16 [3, 3, 64, 64], replicated
- refine_v2: float32 [3, 64], replicated
- down_w3: bfloat16 [3, 3, 64, 128], replicated
- down_v3: float32 [3, 128], replicated
- refine_w3: bfloat16 [3, 3, 128, 128], replicated
- refine_v3: float32 [3, 128], replicated
Outputs:
- output: bfloat16 [512, 16, 32, 128], P('batch', 'h', 'w')
All inputs are finite; a program needn't handle non-finite values.
Results may differ from a plain program's by a relative error of at most 0.00349926.
Values are sent between devices in bfloat16 or wider.
A program may use at most 768 MiB of HBM per device.

v0:
```python
import jax
import jax.numpy as jnp
from jax import lax
from jax.sharding import PartitionSpec as P

NORM_GROUPS = 8
NORM_EPS = 1e-5


def shift_in(piece, axis_name, axis_size, from_lower):
    if axis_size == 1:
        return jnp.zeros_like(piece)
    if from_lower:
        send_pairs = [(source, source + 1) for source in range(axis_size - 1)]
    else:
        send_pairs = [(source + 1, source) for source in range(axis_size - 1)]
    return lax.ppermute(piece, axis_name, send_pairs)


def lower_halo(tile, row_count, col_count):
    above = shift_in(tile[:, -1:], "h", row_count, True)
    tall = jnp.concatenate([above, tile], axis=1)
    left = shift_in(tall[:, :, -1:], "w", col_count, True)
    return jnp.concatenate([left, tall], axis=2)


def both_halo(tile, row_count, col_count):
    above = shift_in(tile[:, -1:], "h", row_count, True)
    below = shift_in(tile[:, :1], "h", row_count, False)
    tall = jnp.concatenate([above, tile, below], axis=1)
    left = shift_in(tall[:, :, -1:], "w", col_count, True)
    right = shift_in(tall[:, :, :1], "w", col_count, False)
    return jnp.concatenate([left, tall, right], axis=2)


def norm_apply(summed, affine, totals, pixel_count, per_group):
    grp_mean = totals[0] / pixel_count
    grp_var = jnp.maximum(totals[1] / pixel_count - jnp.square(grp_mean), 0.0)
    inv_std = lax.rsqrt(grp_var + NORM_EPS)
    chan_scale = jnp.repeat(inv_std, per_group, axis=1) * affine[1]
    chan_shift = affine[2] - jnp.repeat(grp_mean * inv_std, per_group, axis=1) * affine[1]
    return jax.nn.relu(summed * chan_scale[:, None, None, :] + chan_shift[:, None, None, :]).astype(jnp.bfloat16)


def conv_norm(padded, kernel, affine, stride, spatial_devices):
    summed = lax.conv_general_dilated(padded, kernel, (stride, stride), "VALID", dimension_numbers=("NHWC", "HWIO", "NHWC"), preferred_element_type=jnp.float32) + affine[0]
    out_shape = summed.shape
    per_group = out_shape[3] // NORM_GROUPS
    pixel_count = out_shape[1] * out_shape[2] * spatial_devices * per_group
    part_sums = jnp.stack([jnp.sum(summed, axis=(1, 2)), jnp.sum(jnp.square(summed), axis=(1, 2))])
    part_sums = jnp.sum(part_sums.reshape(2, out_shape[0], NORM_GROUPS, per_group), axis=3)
    totals = lax.psum(part_sums, ("h", "w"))
    return norm_apply(summed, affine, totals, pixel_count, per_group)


def solution(mesh):
    row_count = mesh.shape["h"]
    col_count = mesh.shape["w"]
    spatial_devices = row_count * col_count
    act_spec = P("batch", "h", "w")

    def local_forward(tile, *params):
        current = tile
        for stage in range(3):
            down_w, down_v, refine_w, refine_v = params[4 * stage:4 * stage + 4]
            current = conv_norm(lower_halo(current, row_count, col_count), down_w, down_v, 2, spatial_devices)
            current = conv_norm(both_halo(current, row_count, col_count), refine_w, refine_v, 1, spatial_devices)
        return current

    return jax.shard_map(local_forward, mesh=mesh, in_specs=(act_spec,) + (P(),) * 12, out_specs=act_spec, check_vma=False)
```

profile of v0, /device:TPU:97, one launch (start us, length us, event | category | flops | bytes accessed | tf_op | source)
XLA Modules:
  0.0 531.9 jit_solution(8550313095503222173)
XLA Ops:
  1.1 4.6 collective-permute-start
  5.7 3.3 collective-permute-done
  9.1 4.0 constant_dynamic-update-slice_fusion
  13.1 3.8 collective-permute-start.1
  18.3 9.5 %add_reduce_fusion.1 = (f32[512,32]{0,1:T(8,128)S(1)}, f32[512,32]{0,1:T(8,128)S(1)}, f32[512,8,32,32]{0,3,2,1:T(8,128)}) fusion(f32[32]{0:T(128)S(1)} %get-tuple-element.57, bf16[3,3,4,32]{3,2,1,0:T(4,128)(2,1)S(1)} %copy-done.11, bf16[512,17,64,4]{0,3,2,1:T(4,128)(2,1)S(1)} %constant_dynamic-update-slice_fusion, ...), kind=kOutput, calls=%fused_computation.5 | convolution fusion | flops 327786496 | bytes 21436800 | tf_op jit(solution)/shard_map/conv_general_dilated | solution.py:46
  27.9 48.9 %psum.42 = f32[2,512,8]{1,2,0:T(8,128)S(1)} all-reduce(f32[2,512,8]{1,2,0:T(8,128)S(1)} %maximum_reduce_fusion.4), channel_id=1, replica_groups=mesh['batch'=1,'w'=4,'h'=8] {'h','w'}, use_global_device_ids=true, to_apply=%region_3.0 | all-reduce | flops 8192 | bytes 65536 | tf_op jit(solution)/shard_map/psum | solution.py:52
  76.9 7.5 %maximum_convert_fusion.1 = bf16[512,8,32,32]{0,3,2,1:T(8,128)(2,1)S(1)} fusion(f32[512,8,32,32]{0,3,2,1:T(8,128)} %get-tuple-element.71, f32[512,32]{0,1:T(8,128)S(1)} %get-tuple-element.70, f32[512,32]{0,1:T(8,128)S(1)} %get-tuple-element.69, f32[32]{0:T(128)S(1)} %get-tuple-element.57), kind=kLoop, calls=%fused_computation.2 | loop fusion | flops 20971520 | bytes 25297024 | tf_op jit(solution)/shard_map/convert_element_type | solution.py:42
  84.7 3.6 collective-permute-start.2
  88.3 2.0 collective-permute-start.3
  90.3 9.7 %collective-permute-done.2 = bf16[512,1,32,32]{0,3,2,1:T(8,128)(2,1)S(1)} collective-permute-done((bf16[512,1,32,32]{0,3,2,1:T(8,128)(2,1)S(1)}, bf16[512,1,32,32]{0,3,2,1:T(8,128)(2,1)S(1)}, u32[]{:S(2)}, u32[]{:S(2)}) %collective-permute-start.2) | collective-permute-done | bytes 1048608 | tf_op jit(solution)/shard_map/ppermute | solution.py:17
  100.0 4.4 collective-permute-done.3
  107.6 2.6 collective-permute-done.4
  110.2 4.1 collective-permute-done.5
  114.3 16.9 %add_reduce_fusion = (f32[512,32]{0,1:T(8,128)S(1)}, f32[512,32]{0,1:T(8,128)S(1)}, f32[512,8,32,32]{0,3,2,1:T(8,128)}) fusion(f32[32]{0:T(128)S(1)} %get-tuple-element.54, bf16[3,3,32,32]{3,2,1,0:T(8,128)(2,1)S(1)} %copy-done.9, bf16[512,10,1,32]{0,3,2,1:T(8,128)(2,1)S(1)} %collective-permute-done.5, ...), kind=kOutput, calls=%fused_computation.4 | convolution fusion | flops 2454945792 | bytes 28067968 | tf_op jit(solution)/shard_map/conv_general_dilated | solution.py:46
  131.4 48.0 %psum.43 = f32[2,512,8]{1,2,0:T(8,128)S(1)} all-reduce(f32[2,512,8]{1,2,0:T(8,128)S(1)} %maximum_reduce_fusion.5), channel_id=1, replica_groups=mesh['batch'=1,'w'=4,'h'=8] {'h','w'}, use_global_device_ids=true, to_apply=%region_7.8 | all-reduce | flops 8192 | bytes 65536 | tf_op jit(solution)/shard_map/psum | solution.py:52
  179.6 7.5 %maximum_convert_fusion = bf16[512,8,32,32]{0,3,2,1:T(8,128)(2,1)S(1)} fusion(f32[512,8,32,32]{0,3,2,1:T(8,128)} %get-tuple-element.72, f32[512,32]{0,1:T(8,128)S(1)} %get-tuple-element.68, f32[512,32]{0,1:T(8,128)S(1)} %get-tuple-element.67, f32[32]{0:T(128)S(1)} %get-tuple-element.54), kind=kLoop, calls=%fused_computation | loop fusion | flops 20971520 | bytes 25297024 | tf_op jit(solution)/shard_map/convert_element_type | solution.py:42
  189.2 11.7 %collective-permute-done.6 = bf16[512,1,32,32]{0,3,2,1:T(8,128)(2,1)S(1)} collective-permute-done((bf16[512,1,32,32]{0,3,2,1:T(8,128)(2,1)S(1)}, bf16[512,1,32,32]{0,3,2,1:T(8,128)(2,1)S(1)}, u32[]{:S(2)}, u32[]{:S(2)}) %collective-permute-start.6) | collective-permute-done | bytes 1048608 | tf_op jit(solution)/shard_map/ppermute | solution.py:17
  200.9 2.4 collective-permute-start.7
  203.4 3.6 collective-permute-done.7
  207.0 6.5 %add_reduce_fusion.3 = (f32[512,64]{0,1:T(8,128)S(1)}, f32[512,64]{0,1:T(8,128)S(1)}, f32[512,4,16,64]{0,3,2,1:T(8,128)}) fusion(f32[64]{0:T(128)S(1)} %get-tuple-element.51, bf16[3,3,32,64]{3,2,1,0:T(8,128)(2,1)S(1)} %copy-done.10, bf16[512,8,32,32]{0,3,2,1:T(8,128)(2,1)S(1)} %maximum_convert_fusion, ...), kind=kOutput, calls=%fused_computation.27 | convolution fusion | flops 1226014720 | bytes 18419968 | tf_op jit(solution)/shard_map/conv_general_dilated | solution.py:46
  213.6 48.5 %psum.44 = f32[2,512,8]{1,2,0:T(8,128)S(1)} all-reduce(f32[2,512,8]{1,2,0:T(8,128)S(1)} %maximum_reduce_fusion.2), channel_id=1, replica_groups=mesh['batch'=1,'w'=4,'h'=8] {'h','w'}, use_global_device_ids=true, to_apply=%region_11.12 | all-reduce | flops 8192 | bytes 65536 | tf_op jit(solution)/shard_map/psum | solution.py:52
  262.1 4.9 maximum_convert_fusion.3
  267.3 2.3 collective-permute-start.8
  269.6 2.1 collective-permute-start.9
  271.7 9.6 %collective-permute-done.8 = bf16[512,1,16,64]{0,3,2,1:T(8,128)(2,1)S(1)} collective-permute-done((bf16[512,1,16,64]{0,3,2,1:T(8,128)(2,1)S(1)}, bf16[512,1,16,64]{0,3,2,1:T(8,128)(2,1)S(1)}, u32[]{:S(2)}, u32[]{:S(2)}) %collective-permute-start.8) | collective-permute-done | bytes 1048608 | tf_op jit(solution)/shard_map/ppermute | solution.py:17
  281.3 4.6 collective-permute-done.9
  286.0 2.2 collective-permute-start.10
  289.5 3.3 collective-permute-done.10
  292.8 3.9 collective-permute-done.11
  296.7 9.3 %add_reduce_fusion.2 = (f32[512,64]{0,1:T(8,128)S(1)}, f32[512,64]{0,1:T(8,128)S(1)}, f32[512,4,16,64]{0,3,2,1:T(8,128)}) fusion(f32[64]{0:T(128)S(1)} %get-tuple-element.48, bf16[3,3,64,64]{3,2,1,0:T(8,128)(2,1)S(1)} %copy-done.7, bf16[512,6,1,64]{0,3,2,1:T(8,128)(2,1)S(1)} %collective-permute-done.11, ...), kind=kOutput, calls=%fused_computation.26 | convolution fusion | flops 2438397952 | bytes 15802624 | tf_op jit(solution)/shard_map/conv_general_dilated | solution.py:46
  306.1 48.2 %psum.45 = f32[2,512,8]{1,2,0:T(8,128)S(1)} all-reduce(f32[2,512,8]{1,2,0:T(8,128)S(1)} %maximum_reduce_fusion.3), channel_id=1, replica_groups=mesh['batch'=1,'w'=4,'h'=8] {'h','w'}, use_global_device_ids=true, to_apply=%region_15.16 | all-reduce | flops 8192 | bytes 65536 | tf_op jit(solution)/shard_map/psum | solution.py:52
  354.5 5.0 maximum_convert_fusion.2
  359.5 2.2 collective-permute-start.12
  361.7 11.7 %collective-permute-done.12 = bf16[512,1,16,64]{0,3,2,1:T(8,128)(2,1)S(1)} collective-permute-done((bf16[512,1,16,64]{0,3,2,1:T(8,128)(2,1)S(1)}, bf16[512,1,16,64]{0,3,2,1:T(8,128)(2,1)S(1)}, u32[]{:S(2)}, u32[]{:S(2)}) %collective-permute-start.12) | collective-permute-done | bytes 1048608 | tf_op jit(solution)/shard_map/ppermute | solution.py:17
  373.4 2.4 collective-permute-start.13
  375.9 3.9 collective-permute-done.13
  379.8 4.7 add_reduce_fusion.5
  384.9 48.9 %psum.46 = f32[2,512,8]{1,2,0:T(8,128)S(1)} all-reduce(f32[2,512,8]{1,2,0:T(8,128)S(1)} %maximum_reduce_fusion), channel_id=1, replica_groups=mesh['batch'=1,'w'=4,'h'=8] {'h','w'}, use_global_device_ids=true, to_apply=%region_19.20 | all-reduce | flops 8192 | bytes 65536 | tf_op jit(solution)/shard_map/psum | solution.py:52
  434.2 3.0 maximum_convert_fusion.5
  437.4 2.7 collective-permute-start.14
  442.1 9.7 %collective-permute-done.14 = bf16[512,1,8,128]{3,0,2,1:T(8,128)(2,1)S(1)} collective-permute-done((bf16[512,1,8,128]{3,0,2,1:T(8,128)(2,1)S(1)}, bf16[512,1,8,128]{3,0,2,1:T(8,128)(2,1)S(1)}, u32[]{:S(2)}, u32[]{:S(2)}) %collective-permute-start.14) | collective-permute-done | bytes 1048608 | tf_op jit(solution)/shard_map/ppermute | solution.py:17
  451.8 4.7 collective-permute-done.15
  459.7 4.7 collective-permute-done.16
  464.4 3.9 collective-permute-done.17
  468.3 6.7 %add_reduce_fusion.4 = (f32[512,128]{1,0:T(8,128)S(1)}, f32[512,128]{1,0:T(8,128)S(1)}, f32[512,2,8,128]{3,0,2,1:T(8,128)}) fusion(f32[128]{0:T(128)S(1)} %get-tuple-element.42, bf16[3,3,128,128]{3,2,1,0:T(8,128)(2,1)S(1)} %copy-done, bf16[512,4,1,128]{3,0,2,1:T(8,128)(2,1)S(1)} %collective-permute-done.17, ...), kind=kOutput, calls=%fused_computation.62 | convolution fusion | flops 2430468096 | bytes 10256896 | tf_op jit(solution)/shard_map/conv_general_dilated | solution.py:46
  475.5 50.3 %psum.47 = f32[2,512,8]{1,2,0:T(8,128)S(1)} all-reduce(f32[2,512,8]{1,2,0:T(8,128)S(1)} %maximum_reduce_fusion.1), channel_id=1, replica_groups=mesh['batch'=1,'w'=4,'h'=8] {'h','w'}, use_global_device_ids=true, to_apply=%region_23.24 | all-reduce | flops 8192 | bytes 65536 | tf_op jit(solution)/shard_map/psum | solution.py:52
  526.2 3.0 maximum_convert_fusion.4
  529.2 2.7 copy.32
  (89 shorter events, 17.2 us)
Async XLA Ops:
  0.0 468.3 %copy-start = (bf16[3,3,128,128]{3,2,1,0:T(8,128)(2,1)S(1)}, bf16[3,3,128,128]{3,2,1,0:T(8,128)(2,1)}, u32[]{:S(2)}) copy-start(bf16[3,3,128,128]{3,2,1,0:T(8,128)(2,1)} %param.24) | copy-start | bytes 884740
  0.0 16.9 %copy-start.1 = (f32[3,32]{1,0:T(4,128)S(1)}, f32[3,32]{1,0:T(4,128)}, u32[]{:S(2)}) copy-start(f32[3,32]{1,0:T(4,128)} %param.15) | copy-start | bytes 1156
  0.0 18.3 %copy-start.11 = (bf16[3,3,4,32]{3,2,1,0:T(4,128)(2,1)S(1)}, bf16[3,3,4,32]{3,2,1,0:T(4,128)(2,1)}, u32[]{:S(2)}) copy-start(bf16[3,3,4,32]{3,2,1,0:T(4,128)(2,1)} %param.14) | copy-start | bytes 6916
  1.1 7.9 %collective-permute-start = (bf16[512,1,64,4]{0,3,2,1:T(4,128)(2,1)S(1)}, bf16[512,1,64,4]{0,3,2,1:T(4,128)(2,1)S(1)}, u32[]{:S(2)}, u32[]{:S(2)}) collective-permute-start(bf16[512,1,64,4]{0,3,2,1:T(4,128)(2,1)S(1)} %slice.150), channel_id=1, source_target_pairs={{0,1},{1,2},{2,3},{3,4},{4,5},{5,6},{6,7},{8,9},{9,10},{10,11},{11... | collective-permute-start | bytes 786440 | tf_op jit(solution)/shard_map/ppermute | solution.py:17
  13.1 5.1 collective-permute-start.1
  84.5 23.1 %copy-start.2 = (f32[3,32]{1,0:T(4,128)S(1)}, f32[3,32]{1,0:T(4,128)}, u32[]{:S(2)}) copy-start(f32[3,32]{1,0:T(4,128)} %param.17) | copy-start | bytes 1156
  84.5 29.8 %copy-start.9 = (bf16[3,3,32,32]{3,2,1,0:T(8,128)(2,1)S(1)}, bf16[3,3,32,32]{3,2,1,0:T(8,128)(2,1)}, u32[]{:S(2)}) copy-start(bf16[3,3,32,32]{3,2,1,0:T(8,128)(2,1)} %param.16) | copy-start | bytes 55300
  84.7 15.3 %collective-permute-start.2 = (bf16[512,1,32,32]{0,3,2,1:T(8,128)(2,1)S(1)}, bf16[512,1,32,32]{0,3,2,1:T(8,128)(2,1)S(1)}, u32[]{:S(2)}, u32[]{:S(2)}) collective-permute-start(bf16[512,1,32,32]{0,3,2,1:T(8,128)(2,1)S(1)} %get-tuple-element.31), channel_id=1, source_target_pairs={{0,1},{1,2},{2,3},{3,4},{4,5},{5,6},{6,7},{8,9},{9,10},{10,11},{11... | collective-permute-start | bytes 3145736 | tf_op jit(solution)/shard_map/ppermute | solution.py:17
  88.3 16.1 %collective-permute-start.3 = (bf16[512,1,32,32]{0,3,2,1:T(8,128)(2,1)S(1)}, bf16[512,1,32,32]{0,3,2,1:T(8,128)(2,1)S(1)}, u32[]{:S(2)}, u32[]{:S(2)}) collective-permute-start(bf16[512,1,32,32]{0,3,2,1:T(8,128)(2,1)S(1)} %get-tuple-element.32), channel_id=1, source_target_pairs={{1,0},{2,1},{3,2},{4,3},{5,4},{6,5},{7,6},{9,8},{10,9},{11,10},{12... | collective-permute-start | bytes 3145736 | tf_op jit(solution)/shard_map/ppermute | solution.py:17
  104.6 5.6 %collective-permute-start.4 = (bf16[512,10,1,32]{0,3,2,1:T(8,128)(2,1)S(1)}, bf16[512,10,1,32]{0,3,2,1:T(8,128)(2,1)S(1)}, u32[]{:S(2)}, u32[]{:S(2)}) collective-permute-start(bf16[512,10,1,32]{0,3,2,1:T(8,128)(2,1)S(1)} %get-tuple-element.29), channel_id=1, source_target_pairs={{0,8},{8,16},{16,24},{1,9},{9,17},{17,25},{2,10},{10,18},{18,26},{... | collective-permute-start | bytes 983048 | tf_op jit(solution)/shard_map/ppermute | solution.py:17
  106.2 8.1 %collective-permute-start.5 = (bf16[512,10,1,32]{0,3,2,1:T(8,128)(2,1)S(1)}, bf16[512,10,1,32]{0,3,2,1:T(8,128)(2,1)S(1)}, u32[]{:S(2)}, u32[]{:S(2)}) collective-permute-start(bf16[512,10,1,32]{0,3,2,1:T(8,128)(2,1)S(1)} %get-tuple-element.30), channel_id=1, source_target_pairs={{8,0},{16,8},{24,16},{9,1},{17,9},{25,17},{10,2},{18,10},{26,18},{... | collective-permute-start | bytes 983048 | tf_op jit(solution)/shard_map/ppermute | solution.py:17
  187.1 16.3 %copy-start.3 = (f32[3,64]{1,0:T(4,128)S(1)}, f32[3,64]{1,0:T(4,128)}, u32[]{:S(2)}) copy-start(f32[3,64]{1,0:T(4,128)} %param.19) | copy-start | bytes 2308
  187.1 19.9 %copy-start.10 = (bf16[3,3,32,64]{3,2,1,0:T(8,128)(2,1)S(1)}, bf16[3,3,32,64]{3,2,1,0:T(8,128)(2,1)}, u32[]{:S(2)}) copy-start(bf16[3,3,32,64]{3,2,1,0:T(8,128)(2,1)} %param.18) | copy-start | bytes 110596
  187.2 13.7 %collective-permute-start.6 = (bf16[512,1,32,32]{0,3,2,1:T(8,128)(2,1)S(1)}, bf16[512,1,32,32]{0,3,2,1:T(8,128)(2,1)S(1)}, u32[]{:S(2)}, u32[]{:S(2)}) collective-permute-start(bf16[512,1,32,32]{0,3,2,1:T(8,128)(2,1)S(1)} %slice.205), channel_id=1, source_target_pairs={{0,1},{1,2},{2,3},{3,4},{4,5},{5,6},{6,7},{8,9},{9,10},{10,11},{11... | collective-permute-start | bytes 3145736 | tf_op jit(solution)/shard_map/ppermute | solution.py:17
  200.9 6.1 %collective-permute-start.7 = (bf16[512,9,1,32]{0,3,2,1:T(8,128)(2,1)S(1)}, bf16[512,9,1,32]{0,3,2,1:T(8,128)(2,1)S(1)}, u32[]{:S(2)}, u32[]{:S(2)}) collective-permute-start(bf16[512,9,1,32]{0,3,2,1:T(8,128)(2,1)S(1)} %pad_maximum_fusion.10), channel_id=1, source_target_pairs={{0,8},{8,16},{16,24},{1,9},{9,17},{17,25},{2,10},{10,18},{18,26},{... | collective-permute-start | bytes 884744 | tf_op jit(solution)/shard_map/ppermute | solution.py:17
  267.1 22.4 %copy-start.4 = (f32[3,64]{1,0:T(4,128)S(1)}, f32[3,64]{1,0:T(4,128)}, u32[]{:S(2)}) copy-start(f32[3,64]{1,0:T(4,128)} %param.21) | copy-start | bytes 2308
  267.1 29.6 %copy-start.7 = (bf16[3,3,64,64]{3,2,1,0:T(8,128)(2,1)S(1)}, bf16[3,3,64,64]{3,2,1,0:T(8,128)(2,1)}, u32[]{:S(2)}) copy-start(bf16[3,3,64,64]{3,2,1,0:T(8,128)(2,1)} %param.20) | copy-start | bytes 221188
  267.3 14.0 %collective-permute-start.8 = (bf16[512,1,16,64]{0,3,2,1:T(8,128)(2,1)S(1)}, bf16[512,1,16,64]{0,3,2,1:T(8,128)(2,1)S(1)}, u32[]{:S(2)}, u32[]{:S(2)}) collective-permute-start(bf16[512,1,16,64]{0,3,2,1:T(8,128)(2,1)S(1)} %get-tuple-element.37), channel_id=1, source_target_pairs={{0,1},{1,2},{2,3},{3,4},{4,5},{5,6},{6,7},{8,9},{9,10},{10,11},{11... | collective-permute-start | bytes 3145736 | tf_op jit(solution)/shard_map/ppermute | solution.py:17
  269.6 16.3 %collective-permute-start.9 = (bf16[512,1,16,64]{0,3,2,1:T(8,128)(2,1)S(1)}, bf16[512,1,16,64]{0,3,2,1:T(8,128)(2,1)S(1)}, u32[]{:S(2)}, u32[]{:S(2)}) collective-permute-start(bf16[512,1,16,64]{0,3,2,1:T(8,128)(2,1)S(1)} %get-tuple-element.38), channel_id=1, source_target_pairs={{1,0},{2,1},{3,2},{4,3},{5,4},{6,5},{7,6},{9,8},{10,9},{11,10},{12... | collective-permute-start | bytes 3145736 | tf_op jit(solution)/shard_map/ppermute | solution.py:17
  286.0 6.8 %collective-permute-start.10 = (bf16[512,6,1,64]{0,3,2,1:T(8,128)(2,1)S(1)}, bf16[512,6,1,64]{0,3,2,1:T(8,128)(2,1)S(1)}, u32[]{:S(2)}, u32[]{:S(2)}) collective-permute-start(bf16[512,6,1,64]{0,3,2,1:T(8,128)(2,1)S(1)} %get-tuple-element.33), channel_id=1, source_target_pairs={{0,8},{8,16},{16,24},{1,9},{9,17},{17,25},{2,10},{10,18},{18,26},{... | collective-permute-start | bytes 1179656 | tf_op jit(solution)/shard_map/ppermute | solution.py:17
  288.2 8.6 %collective-permute-start.11 = (bf16[512,6,1,64]{0,3,2,1:T(8,128)(2,1)S(1)}, bf16[512,6,1,64]{0,3,2,1:T(8,128)(2,1)S(1)}, u32[]{:S(2)}, u32[]{:S(2)}) collective-permute-start(bf16[512,6,1,64]{0,3,2,1:T(8,128)(2,1)S(1)} %get-tuple-element.34), channel_id=1, source_target_pairs={{8,0},{16,8},{24,16},{9,1},{17,9},{25,17},{10,2},{18,10},{26,18},{... | collective-permute-start | bytes 1179656 | tf_op jit(solution)/shard_map/ppermute | solution.py:17
  354.5 21.4 %copy-start.5 = (f32[3,128]{1,0:T(4,128)S(1)}, f32[3,128]{1,0:T(4,128)}, u32[]{:S(2)}) copy-start(f32[3,128]{1,0:T(4,128)} %param.23) | copy-start | bytes 4612
  354.5 25.4 %copy-start.8 = (bf16[3,3,64,128]{3,2,1,0:T(8,128)(2,1)S(1)}, bf16[3,3,64,128]{3,2,1,0:T(8,128)(2,1)}, u32[]{:S(2)}) copy-start(bf16[3,3,64,128]{3,2,1,0:T(8,128)(2,1)} %param.22) | copy-start | bytes 442372
  359.5 13.9 %collective-permute-start.12 = (bf16[512,1,16,64]{0,3,2,1:T(8,128)(2,1)S(1)}, bf16[512,1,16,64]{0,3,2,1:T(8,128)(2,1)S(1)}, u32[]{:S(2)}, u32[]{:S(2)}) collective-permute-start(bf16[512,1,16,64]{0,3,2,1:T(8,128)(2,1)S(1)} %slice.212), channel_id=1, source_target_pairs={{0,1},{1,2},{2,3},{3,4},{4,5},{5,6},{6,7},{8,9},{9,10},{10,11},{11... | collective-permute-start | bytes 3145736 | tf_op jit(solution)/shard_map/ppermute | solution.py:17
  373.4 6.4 %collective-permute-start.13 = (bf16[512,5,1,64]{0,3,2,1:T(8,128)(2,1)S(1)}, bf16[512,5,1,64]{0,3,2,1:T(8,128)(2,1)S(1)}, u32[]{:S(2)}, u32[]{:S(2)}) collective-permute-start(bf16[512,5,1,64]{0,3,2,1:T(8,128)(2,1)S(1)} %pad_maximum_fusion.6), channel_id=1, source_target_pairs={{0,8},{8,16},{16,24},{1,9},{9,17},{17,25},{2,10},{10,18},{18,26},{... | collective-permute-start | bytes 983048 | tf_op jit(solution)/shard_map/ppermute | solution.py:17
  434.2 25.5 %copy-start.6 = (f32[3,128]{1,0:T(4,128)S(1)}, f32[3,128]{1,0:T(4,128)}, u32[]{:S(2)}) copy-start(f32[3,128]{1,0:T(4,128)} %param.25) | copy-start | bytes 4612
  437.4 14.4 %collective-permute-start.14 = (bf16[512,1,8,128]{3,0,2,1:T(8,128)(2,1)S(1)}, bf16[512,1,8,128]{3,0,2,1:T(8,128)(2,1)S(1)}, u32[]{:S(2)}, u32[]{:S(2)}) collective-permute-start(bf16[512,1,8,128]{3,0,2,1:T(8,128)(2,1)S(1)} %get-tuple-element.39), channel_id=1, source_target_pairs={{0,1},{1,2},{2,3},{3,4},{4,5},{5,6},{6,7},{8,9},{9,10},{10,11},{11... | collective-permute-start | bytes 3145736 | tf_op jit(solution)/shard_map/ppermute | solution.py:17
  440.1 16.4 %collective-permute-start.15 = (bf16[512,1,8,128]{3,0,2,1:T(8,128)(2,1)S(1)}, bf16[512,1,8,128]{3,0,2,1:T(8,128)(2,1)S(1)}, u32[]{:S(2)}, u32[]{:S(2)}) collective-permute-start(bf16[512,1,8,128]{3,0,2,1:T(8,128)(2,1)S(1)} %get-tuple-element.40), channel_id=1, source_target_pairs={{1,0},{2,1},{3,2},{4,3},{5,4},{6,5},{7,6},{9,8},{10,9},{11,10},{12... | collective-permute-start | bytes 3145736 | tf_op jit(solution)/shard_map/ppermute | solution.py:17
  456.7 7.8 %collective-permute-start.16 = (bf16[512,4,1,128]{3,0,2,1:T(8,128)(2,1)S(1)}, bf16[512,4,1,128]{3,0,2,1:T(8,128)(2,1)S(1)}, u32[]{:S(2)}, u32[]{:S(2)}) collective-permute-start(bf16[512,4,1,128]{3,0,2,1:T(8,128)(2,1)S(1)} %get-tuple-element.35), channel_id=1, source_target_pairs={{0,8},{8,16},{16,24},{1,9},{9,17},{17,25},{2,10},{10,18},{18,26},{... | collective-permute-start | bytes 1572872 | tf_op jit(solution)/shard_map/ppermute | solution.py:17
  458.4 10.0 %collective-permute-start.17 = (bf16[512,4,1,128]{3,0,2,1:T(8,128)(2,1)S(1)}, bf16[512,4,1,128]{3,0,2,1:T(8,128)(2,1)S(1)}, u32[]{:S(2)}, u32[]{:S(2)}) collective-permute-start(bf16[512,4,1,128]{3,0,2,1:T(8,128)(2,1)S(1)} %get-tuple-element.36), channel_id=1, source_target_pairs={{8,0},{16,8},{24,16},{9,1},{17,9},{25,17},{10,2},{18,10},{26,18},{... | collective-permute-start | bytes 1572872 | tf_op jit(solution)/shard_map/ppermute | solution.py:17
where the time goes:
time: 533 us; the launch traced here: 532 us
  blocking collectives  293 us (55%)
  waiting for transfers between devices  101 us (19%)
  matrix products  53.7 us (10%)
  starting transfers between devices  41.4 us (8%)
  other arithmetic  32.3 us (6%)
  local copies, waits for them, and re-layouts  9.93 us (2%)
    psum x6, blocking collectives, conv_norm(): totals = lax.psum(part_sums, ('h', 'w'))  293 us
    ppermute x18, waiting for transfers between devices, shift_in(): return lax.ppermute(piece, axis_name, send_pairs)  101 us
    conv_general_dilated x6, matrix products, conv_norm(): lax.conv_general_dilated(padded, kernel, (stride, stride), 'VALID', dimen...  53.7 us
    ppermute x18, starting transfers between devices, shift_in(): return lax.ppermute(piece, axis_name, send_pairs)  41.4 us
    convert_element_type x6, other arithmetic, norm_apply(): jax.nn.relu(summed * chan_scale[:, None, None, :] + chan_shift[:, None, N...  30.8 us
  transfers between devices with their start and end apart: 18, of which 18 were waited for; matrix products, arithmetic and copies ran while one was open for 0% of the time, Pallas kernels for 0%

commit v1 on v0

v1 whole, which is shorter than its diff:
```python
import functools

import jax
import jax.numpy as jnp
from jax import lax
from jax.experimental import pallas as pl
from jax.experimental.pallas import tpu as pltpu
from jax.sharding import PartitionSpec as P

NORM_GROUPS = 8
NORM_EPS = 1e-5
CHUNKS = 2
BLOCKS = ((2, 1, 8), (1, 2, 4), (2, 1, 2), (1, 2, 2), (2, 1, 2), (1, 1, 2))


def patch_shape(stride, bh, bw, first):
    rows = (bh - 1) * stride + 3
    cols = (bw - 1) * stride + 3
    if first:
        cols = bw * stride + 4
    return rows, cols


def block_weights(kernel, stride, bh, bw, first):
    rows, cols = patch_shape(stride, bh, bw, first)
    off = 3 if first else 0
    flipped = kernel.transpose(3, 0, 1, 2)
    parts = []
    for i in range(bh):
        for j in range(bw):
            top, left = stride * i, off + stride * j
            padded = jnp.pad(flipped, ((0, 0), (top, rows - 3 - top), (left, cols - 3 - left), (0, 0)))
            parts.append(padded.reshape(kernel.shape[3], -1))
    return jnp.concatenate(parts, axis=0)


def encoder_kernel(cfg, x_ref, *refs):
    th, tw, c0, widths, grid_h, grid_w, imgs = cfg
    tiles = grid_h * grid_w
    lanes = tiles * imgs
    w_refs, v_refs = refs[0:6], refs[6:12]
    out_ref = refs[12]
    xp, acc_a, y1, z1, y2, z2, y3, s_ref = refs[13:]

    def iota(shape, dim):
        return lax.broadcasted_iota(jnp.int32, shape, dim)

    src = iota((lanes, lanes), 0)
    dst = iota((lanes, lanes), 1)

    def perm(dh, dw):
        t = dst // imgs
        h, w = t % grid_h + dh, t // grid_h + dw
        inside = (h >= 0) & (h < grid_h) & (w >= 0) & (w < grid_w)
        want = (w * grid_h + h) * imgs + dst % imgs
        return jnp.where(inside & (src == want), 1.0, 0.0).astype(jnp.bfloat16)

    above, below, left, right = perm(-1, 0), perm(1, 0), perm(0, -1), perm(0, 1)
    same_image = jnp.where(src % imgs == dst % imgs, 1.0, 0.0)

    def move(value, matrix):
        return jnp.dot(value, matrix, preferred_element_type=jnp.float32).astype(jnp.bfloat16)

    def halos(buf, rows, cols, unit, both):
        buf[0] = move(buf[rows], above)
        if both:
            buf[rows + 1] = move(buf[1], below)
        for r in range(rows + (2 if both else 1)):
            buf[r, 0:unit] = move(buf[r, cols * unit:(cols + 1) * unit], left)
            if both:
                buf[r, (cols + 1) * unit:(cols + 2) * unit] = move(buf[r, unit:2 * unit], right)

    def conv(buf, w_ref, stride, bh, bw, ci, co, out_h, out_w, first):
        rows, cols = patch_shape(stride, bh, bw, first)
        s_ref[:, 0:co] = jnp.zeros((2, co, lanes), jnp.float32)

        def row_body(i, carry):
            for j in range(out_w // bw):
                start = j * bw * stride * ci
                patch = jnp.concatenate([buf[i * (bh * stride) + r, start:start + cols * ci] for r in range(rows)], axis=0)
                res = jnp.dot(w_ref[...], patch, preferred_element_type=jnp.float32)
                parts = [res[p * co:(p + 1) * co] for p in range(bh * bw)]
                s_ref[0, 0:co] += functools.reduce(jnp.add, parts)
                s_ref[1, 0:co] += functools.reduce(jnp.add, [p * p for p in parts])
                for b in range(bh):
                    acc_a[i * bh + b, j * bw * co:(j + 1) * bw * co] = res[b * bw * co:(b + 1) * bw * co]
            return carry

        lax.fori_loop(0, out_h // bh, row_body, 0)

    def stats(v_ref, co, pixels):
        per = co // NORM_GROUPS
        group = jnp.where(iota((co, co), 0) // per == iota((co, co), 1) // per, 1.0, 0.0)
        hi = lax.Precision.HIGHEST
        tot = jnp.dot(s_ref[:, 0:co].reshape(2 * co, lanes), same_image, precision=hi, preferred_element_type=jnp.float32) / pixels
        mean_c, sq_c = tot[0:co], tot[co:2 * co]
        var_c = jnp.maximum(sq_c - mean_c * mean_c, 0.0)
        bias, gain, shift = v_ref[:, 0:1], v_ref[:, 1:2], v_ref[:, 2:3]
        mean_a = mean_c + bias
        m = jnp.dot(group, mean_a, precision=hi, preferred_element_type=jnp.float32) / per
        dev = mean_a - m
        q = jnp.dot(group, var_c + dev * dev, precision=hi, preferred_element_type=jnp.float32) / per
        scale = lax.rsqrt(q + NORM_EPS) * gain
        return scale, shift + (bias - m) * scale

    def normalise(scale, offset, co, out_h, out_w, dst_buf):
        def row_body(i, carry):
            for j in range(out_w):
                val = acc_a[i, j * co:(j + 1) * co]
                dst_buf[i + 1, (j + 1) * co:(j + 2) * co] = jnp.maximum(val * scale + offset, 0.0).astype(jnp.bfloat16)
            return carry

        lax.fori_loop(0, out_h, row_body, 0)

    width0 = tw * c0
    unit0 = 4 * c0

    def load_body(r, carry):
        block = x_ref[:, pl.ds(pl.multiple_of(r * width0, width0), width0)]
        xp[r + 1, unit0:unit0 + width0] = block.T
        return carry

    lax.fori_loop(0, th, load_body, 0)
    xp[0, unit0:unit0 + width0] = move(xp[th, unit0:unit0 + width0], above)
    for r in range(th + 1):
        xp[r, 0:unit0] = move(xp[r, width0:width0 + unit0], left)

    bufs = (xp, y1, z1, y2, z2, y3, None)
    h, w, ci = th, tw, c0
    for layer in range(6):
        stride, bh, bw = BLOCKS[layer]
        co = widths[layer // 2]
        h, w = h // stride, w // stride
        conv(bufs[layer], w_refs[layer], stride, bh, bw, ci, co, h, w, layer == 0)
        scale, offset = stats(v_refs[layer], co, float(h * w * tiles))
        ci = co
        if layer < 5:
            normalise(scale, offset, co, h, w, bufs[layer + 1])
            halos(bufs[layer + 1], h, w, co, layer % 2 == 0)
        else:
            for i in range(h):
                for j in range(w):
                    val = jnp.maximum(acc_a[i, j * co:(j + 1) * co] * scale + offset, 0.0)
                    out_ref[:, i * w + j] = val.T.reshape(tiles, imgs, co).astype(jnp.bfloat16)


def pack_kernel(x_ref, out_ref):
    rows, tw, c0, count = x_ref.shape
    for r in range(rows):
        out_ref[:, r * tw * c0:(r + 1) * tw * c0] = x_ref[r].reshape(tw * c0, count).T


def pack(tile):
    count, th, tw, c0 = tile.shape
    return pl.pallas_call(
        pack_kernel,
        grid=(th // 2,),
        out_shape=jax.ShapeDtypeStruct((count, th * tw * c0), tile.dtype),
        in_specs=[pl.BlockSpec((2, tw, c0, count), lambda r: (r, 0, 0, 0))],
        out_specs=pl.BlockSpec((count, 2 * tw * c0), lambda r: (0, r)),
    )(tile.transpose(1, 2, 3, 0))


def encode(cfg, x, weights, affines):
    th, tw, c0, widths, grid_h, grid_w, imgs = cfg
    tiles = grid_h * grid_w
    lanes = tiles * imgs
    c1, c2, c3 = widths
    bf16, f32 = jnp.bfloat16, jnp.float32
    vmem = pl.BlockSpec(memory_space=pltpu.VMEM)
    h1, w1, h2, w2, h3, w3 = th // 2, tw // 2, th // 4, tw // 4, th // 8, tw // 8
    flops = 2 * 9 * lanes * (h1 * w1 * (c0 * c1 + c1 * c1) + h2 * w2 * (c1 * c2 + c2 * c2) + h3 * w3 * (c2 * c3 + c3 * c3)) * 4
    return pl.pallas_call(
        functools.partial(encoder_kernel, cfg),
        out_shape=jax.ShapeDtypeStruct((tiles, h3 * w3, imgs, c3), bf16),
        in_specs=[vmem] * 13,
        out_specs=vmem,
        scratch_shapes=[
            pltpu.VMEM((th + 1, (tw + 4) * c0, lanes), bf16),
            pltpu.VMEM((h1, w1 * c1, lanes), f32),
            pltpu.VMEM((h1 + 2, (w1 + 2) * c1, lanes), bf16),
            pltpu.VMEM((h1 + 1, (w1 + 1) * c1, lanes), bf16),
            pltpu.VMEM((h2 + 2, (w2 + 2) * c2, lanes), bf16),
            pltpu.VMEM((h2 + 1, (w2 + 1) * c2, lanes), bf16),
            pltpu.VMEM((h3 + 2, (w3 + 2) * c3, lanes), bf16),
            pltpu.VMEM((2, c3, lanes), f32),
        ],
        compiler_params=pltpu.CompilerParams(vmem_limit_bytes=60 * 1024 * 1024),
        cost_estimate=pl.CostEstimate(flops=flops, bytes_accessed=4 * 1024 * 1024, transcendentals=0),
    )(x, *weights, *affines)


def solution(mesh):
    grid_h = mesh.shape["h"]
    grid_w = mesh.shape["w"]
    tiles = grid_h * grid_w
    act_spec = P("batch", "h", "w")

    def local_forward(tile, *params):
        count, th, tw, c0 = tile.shape
        kernels, affines = params[0::2], params[1::2]
        widths = tuple(kernels[2 * s].shape[3] for s in range(3))
        weights = [block_weights(k, *BLOCKS[i], i == 0) for i, k in enumerate(kernels)]
        columns = [v.T for v in affines]
        imgs = count // tiles // CHUNKS
        cfg = (th, tw, c0, widths, grid_h, grid_w, imgs)
        rows = pack(tile).reshape(CHUNKS, tiles, imgs, th * tw * c0)
        outs = []
        for k in range(CHUNKS):
            got = lax.all_to_all(rows[k], ("w", "h"), 0, 0)
            res = encode(cfg, got.reshape(tiles * imgs, th * tw * c0), weights, columns)
            outs.append(lax.all_to_all(res, ("w", "h"), 0, 0))
        full = jnp.stack(outs)
        return full.transpose(0, 1, 3, 2, 4).reshape(count, th // 8, tw // 8, widths[2])

    return jax.shard_map(local_forward, mesh=mesh, in_specs=(act_spec,) + (P(),) * 12, out_specs=act_spec, check_vma=False)
```

time: 533 us -> 182 us (0.34)
  blocking collectives: 293 us -> 22.9 us
  waiting for transfers between devices: 101 us -> 0.01 us
  Pallas kernels: 0 us -> 73.7 us
  matrix products: 53.7 us -> 0 us
  local copies, waits for them, and re-layouts: 9.93 us -> 56 us
  other arithmetic: 32.3 us -> 5.41 us
  starting transfers between devices: 41.4 us -> 21.8 us
    psum x6 -> x0, blocking collectives: 293 us -> none  [conv_norm(): totals = lax.psum(part_sums, ('h', 'w'))]
    ppermute x18 -> x0, waiting for transfers between devices: 101 us -> none  [shift_in(): return lax.ppermute(piece, axis_name, send_pairs)]
    pallas_call x0 -> x3, Pallas kernels: none -> 73.7 us  [the longest x2 66.4 us: encode(): pl.pallas_call(functools.partial(encoder_kernel, cfg), out_shape=jax.Shap...]
    conv_general_dilated x6 -> x0, matrix products: 53.7 us -> none  [conv_norm(): lax.conv_general_dilated(padded, kernel, (stride, stride), 'VALID', dimen...]
    ppermute x18 -> x0, starting transfers between devices: 41.4 us -> none  [shift_in(): return lax.ppermute(piece, axis_name, send_pairs)]
    convert_element_type x6 -> x0, other arithmetic: 30.8 us -> none  [norm_apply(): jax.nn.relu(summed * chan_scale[:, None, None, :] + chan_shift[:, None, N...]
    reshape x4 -> x26, local copies, waits for them, and re-layouts: 0.1 us -> 23.7 us  [block_weights(): parts.append(padded.reshape(kernel.shape[3], -1))]
    all_to_all x0 -> x1, blocking collectives: none -> 22.9 us  [local_forward(): outs.append(lax.all_to_all(res, ('w', 'h'), 0, 0))]
  transfers between devices with their start and end apart: 18 -> 3, of which waited for: 18 -> 0; matrix products, arithmetic and copies ran while one was open for 0% -> 30% of each run, Pallas kernels for 0% -> 37%
where the time goes in v1:
time: 182 us; the launch traced here: 180 us
  Pallas kernels  73.7 us (40%)
  local copies, waits for them, and re-layouts  56 us (31%)
  blocking collectives  22.9 us (13%)
  starting transfers between devices  21.8 us (12%)
  other arithmetic  5.41 us (3%)
    pallas_call x2, Pallas kernels, encode(): pl.pallas_call(functools.partial(encoder_kernel, cfg), out_shape=jax.Shap...  66.4 us
    reshape x26, local copies, waits for them, and re-layouts, block_weights(): parts.append(padded.reshape(kernel.shape[3], -1))  23.7 us
    all_to_all x1, blocking collectives, local_forward(): outs.append(lax.all_to_all(res, ('w', 'h'), 0, 0))  22.9 us
    unnamed x50, local copies, waits for them, and re-layouts  18.4 us
    all_to_all x2, starting transfers between devices, local_forward(): got = lax.all_to_all(rows[k], ('w', 'h'), 0, 0)  15.5 us
    pallas_call x1, Pallas kernels, pack(): pl.pallas_call(pack_kernel, grid=(th // 2,), out_shape=jax.ShapeDtypeStru...  7.28 us
    all_to_all x1, starting transfers between devices, local_forward(): outs.append(lax.all_to_all(res, ('w', 'h'), 0, 0))  6.3 us
    pad x6, local copies, waits for them, and re-layouts, block_weights(): jnp.pad(flipped, ((0, 0), (top, rows - 3 - top), (left, cols - 3 - left),...  5.79 us
  transfers between devices with their start and end apart: 3, of which 0 were waited for; matrix products, arithmetic and copies ran while one was open for 30% of the time, Pallas kernels for 37%

profile of v1, /device:TPU:97, one launch (start us, length us, event | category | flops | bytes accessed | tf_op | source)
XLA Modules:
  0.0 180.0 jit_solution(6837699270882331902)
XLA Ops:
  0.0 7.3 %shard_map.127 = bf16[512,4096]{1,0:T(8,128)(2,1)} custom-call(bf16[16,64,4,512]{3,2,1,0:T(4,128)(2,1)} %bitcast.50), custom_call_target="tpu_custom_call" | custom-call | tf_op jit(solution)/shard_map/pallas_call | solution.py:155
  7.3 4.8 %slice_bitcast_fusion.1 = (bf16[32,8,4096]{2,1,0:T(8,128)(2,1)}, bf16[32,8,4096]{2,1,0:T(8,128)(2,1)}) fusion(bf16[512,4096]{1,0:T(8,128)(2,1)} %shard_map.127), kind=kLoop, calls=%fused_computation.1 | loop fusion | bytes 8388608 | tf_op jit(solution)/shard_map/squeeze | solution.py:210
  12.0 9.1 %all-to-all-start.2 = ((bf16[32,8,4096]{2,1,0:T(8,128)(2,1)}), bf16[32,8,4096]{2,1,0:T(8,128)(2,1)S(1)}, u32[]{:S(2)}, u32[]{:S(2)}) async-start(bf16[32,8,4096]{2,1,0:T(8,128)(2,1)} %get-tuple-element.6), calls=%async_computation.2 | async-start | bytes 4194304 | tf_op jit(solution)/shard_map/all_to_all | solution.py:210
  21.2 0.8 fusion.5
  22.9 1.3 fusion.4
  24.9 0.8 fusion.1
  25.7 1.1 fusion
  28.0 1.5 copy.49
  29.5 1.5 copy.50
  31.0 1.5 copy.51
  32.5 1.5 copy.52
  34.1 1.7 copy.79
  35.8 1.7 copy.80
  37.5 1.6 copy.81
  39.1 1.7 copy.82
  40.8 1.7 copy.83
  42.4 1.7 copy.84
  44.1 1.7 copy.85
  45.7 0.7 copy.86
  46.5 1.6 copy.63
  48.8 1.1 copy.69
  49.9 0.8 copy.68
  51.1 1.4 constant_dynamic-update-slice_fusion.4
  52.4 1.3 constant_dynamic-update-slice_fusion.3
  53.8 1.3 constant_dynamic-update-slice_fusion.2
  55.1 1.3 constant_dynamic-update-slice_fusion.1
  56.4 0.8 constant_dynamic-update-slice_fusion.15
  57.2 0.8 constant_dynamic-update-slice_fusion.14
  58.0 0.8 constant_dynamic-update-slice_fusion.13
  58.8 0.8 constant_dynamic-update-slice_fusion.12
  59.6 0.8 constant_dynamic-update-slice_fusion.11
  60.4 0.8 constant_dynamic-update-slice_fusion.10
  61.2 0.8 constant_dynamic-update-slice_fusion.9
  62.0 0.8 constant_dynamic-update-slice_fusion.8.refs_1_
  62.8 1.7 pad_maximum_fusion.3.refs_2_
  64.5 1.8 pad_maximum_fusion.2.refs_4_
  66.3 1.1 fusion.2
  67.3 0.9 pad_maximum_fusion.refs_5_
  68.3 1.3 copy-done
  69.7 6.3 %all-to-all-start = ((bf16[32,8,4096]{2,1,0:T(8,128)(2,1)}), bf16[32,8,4096]{2,1,0:T(8,128)(2,1)}, u32[]{:S(2)}, u32[]{:S(2)}) async-start(bf16[32,8,4096]{2,1,0:T(8,128)(2,1)} %get-tuple-element.5), calls=%async_computation | async-start | bytes 4194304 | tf_op jit(solution)/shard_map/all_to_all | solution.py:210
  80.0 0.7 copy.76
  80.7 0.7 copy.77
  81.4 0.8 pad_maximum_fusion.1.refs_3_
  82.3 33.2 %shard_map.129 = bf16[32,16,8,128]{3,2,1,0:T(8,128)(2,1)} custom-call(bf16[256,4096]{1,0:T(8,128)(2,1)} %bitcast.53, bf16[256,240]{1,0:T(8,128)(2,1)} %constant_dynamic-update-slice_fusion.refs_0_, bf16[256,768]{1,0:T(8,128)(2,1)} %copy-done.8, bf16[128,480]{1,0:T(8,128)(2,1)} %pad_maximum_fusion.3.refs_2_, bf16[256,1024]{1,0:T(8,128)(2,1)} %pad_maximum_fusion.1.refs_3_, ...), custom_call_target="tpu_custom_call" | custom-call | flops 19931332608 | bytes 4194304 | tf_op jit(solution)/shard_map/pallas_call | solution.py:173
  115.5 6.3 %all-to-all-start.3 = ((bf16[32,16,8,128]{3,2,1,0:T(8,128)(2,1)}), bf16[32,16,8,128]{3,2,1,0:T(8,128)(2,1)S(1)}, u32[]{:S(2)}, u32[]{:S(2)}) async-start(bf16[32,16,8,128]{3,2,1,0:T(8,128)(2,1)} %shard_map.129), calls=%async_computation.3 | async-start | bytes 2097152 | tf_op jit(solution)/shard_map/all_to_all | solution.py:212
  121.8 33.2 %shard_map.128 = bf16[32,16,8,128]{3,2,1,0:T(8,128)(2,1)} custom-call(bf16[256,4096]{1,0:T(8,128)(2,1)} %bitcast.2.x_ref, bf16[256,240]{1,0:T(8,128)(2,1)} %constant_dynamic-update-slice_fusion.refs_0_, bf16[256,768]{1,0:T(8,128)(2,1)} %copy-done.8, bf16[128,480]{1,0:T(8,128)(2,1)} %pad_maximum_fusion.3.refs_2_, ...), custom_call_target="tpu_custom_call" | custom-call | flops 19931332608 | bytes 4194304 | tf_op jit(solution)/shard_map/pallas_call | solution.py:173
  155.0 22.9 %all_to_all.20 = bf16[32,16,8,128]{3,2,1,0:T(8,128)(2,1)S(1)} all-to-all(bf16[32,16,8,128]{3,2,1,0:T(8,128)(2,1)} %shard_map.128), channel_id=1, replica_groups=mesh['batch'=1,'w'=4,'h'=8] {'w','h'}, dimensions={0} | all-to-all | bytes 2097152 | tf_op jit(solution)/shard_map/all_to_all | solution.py:212
  178.1 2.0 %copy.78 = bf16[2,32,8,16,128]{4,3,2,1,0:T(8,128)(2,1)} copy(bf16[2,32,8,16,128]{4,2,3,1,0:T(8,128)(2,1)S(1)} %maximum_bitcast_fusion) | data formatting | bytes 4194304 | tf_op jit(solution)/shard_map/transpose | solution.py:214
  (53 shorter events, 8.1 us)
Async XLA Ops:
  12.0 9.2 %copy-start.7 = (bf16[3,3,4,32]{3,2,1,0:T(4,128)(2,1)S(1)}, bf16[3,3,4,32]{3,2,1,0:T(4,128)(2,1)}, u32[]{:S(2)}) copy-start(bf16[3,3,4,32]{3,2,1,0:T(4,128)(2,1)} %param.14) | copy-start | bytes 6916
  12.0 10.9 %copy-start.5 = (bf16[3,3,32,32]{3,2,1,0:T(8,128)(2,1)S(1)}, bf16[3,3,32,32]{3,2,1,0:T(8,128)(2,1)}, u32[]{:S(2)}) copy-start(bf16[3,3,32,32]{3,2,1,0:T(8,128)(2,1)} %param.16) | copy-start | bytes 55300
  12.0 56.2 %all-to-all-start.2 = ((bf16[32,8,4096]{2,1,0:T(8,128)(2,1)}), bf16[32,8,4096]{2,1,0:T(8,128)(2,1)S(1)}, u32[]{:S(2)}, u32[]{:S(2)}) async-start(bf16[32,8,4096]{2,1,0:T(8,128)(2,1)} %get-tuple-element.6), calls=%async_computation.2 | async-start | bytes 4194304 | tf_op jit(solution)/shard_map/all_to_all | solution.py:210
  21.2 3.0 %copy-start.6 = (bf16[3,3,32,64]{3,2,1,0:T(8,128)(2,1)S(1)}, bf16[3,3,32,64]{3,2,1,0:T(8,128)(2,1)}, u32[]{:S(2)}) copy-start(bf16[3,3,32,64]{3,2,1,0:T(8,128)(2,1)} %param.18) | copy-start | bytes 110596
  21.2 3.7 %copy-start.4 = (bf16[3,3,64,128]{3,2,1,0:T(8,128)(2,1)S(1)}, bf16[3,3,64,128]{3,2,1,0:T(8,128)(2,1)}, u32[]{:S(2)}) copy-start(bf16[3,3,64,128]{3,2,1,0:T(8,128)(2,1)} %param.22) | copy-start | bytes 442372
  51.1 15.2 %copy-start.3 = (bf16[3,3,64,64]{3,2,1,0:T(8,128)(2,1)S(1)}, bf16[3,3,64,64]{3,2,1,0:T(8,128)(2,1)}, u32[]{:S(2)}) copy-start(bf16[3,3,64,64]{3,2,1,0:T(8,128)(2,1)} %param.20) | copy-start | bytes 221188
  62.8 3.5 %copy-start.8 = (bf16[256,768]{1,0:T(8,128)(2,1)}, bf16[256,768]{1,0:T(8,128)(2,1)S(1)}, u32[]{:S(2)}) copy-start(bf16[256,768]{1,0:T(8,128)(2,1)S(1)} %constant_dynamic-update-slice_fusion.8.refs_1_) | copy-start | bytes 1179652
  68.3 1.4 copy-start
  68.3 8.4 %copy-start.2 = (bf16[64,4,4,64]{0,3,2,1:T(8,128)(2,1)S(1)}, bf16[64,4,4,64]{0,3,2,1:T(8,128)(2,1)}, u32[]{:S(2)}) copy-start(bf16[64,4,4,64]{0,3,2,1:T(8,128)(2,1)} %get-tuple-element.12) | copy-start | bytes 393220
  68.3 8.5 %copy-start.1 = (bf16[64,4,4,64]{0,3,2,1:T(8,128)(2,1)S(1)}, bf16[64,4,4,64]{0,3,2,1:T(8,128)(2,1)}, u32[]{:S(2)}) copy-start(bf16[64,4,4,64]{0,3,2,1:T(8,128)(2,1)} %get-tuple-element.13) | copy-start | bytes 393220
  68.3 8.9 %copy-start.9 = (f32[3,32]{1,0:T(4,128)S(1)}, f32[3,32]{1,0:T(4,128)}, u32[]{:S(2)}) copy-start(f32[3,32]{1,0:T(4,128)} %param.15) | copy-start | bytes 1156
  68.3 9.6 %copy-start.10 = (f32[3,32]{1,0:T(4,128)S(1)}, f32[3,32]{1,0:T(4,128)}, u32[]{:S(2)}) copy-start(f32[3,32]{1,0:T(4,128)} %param.17) | copy-start | bytes 1156
  68.3 10.3 %copy-start.11 = (f32[3,64]{1,0:T(4,128)S(1)}, f32[3,64]{1,0:T(4,128)}, u32[]{:S(2)}) copy-start(f32[3,64]{1,0:T(4,128)} %param.19) | copy-start | bytes 2308
  68.3 11.0 %copy-start.12 = (f32[3,64]{1,0:T(4,128)S(1)}, f32[3,64]{1,0:T(4,128)}, u32[]{:S(2)}) copy-start(f32[3,64]{1,0:T(4,128)} %param.21) | copy-start | bytes 2308
  68.3 11.7 %copy-start.13 = (f32[3,128]{1,0:T(4,128)S(1)}, f32[3,128]{1,0:T(4,128)}, u32[]{:S(2)}) copy-start(f32[3,128]{1,0:T(4,128)} %param.23) | copy-start | bytes 4612
  68.3 12.4 %copy-start.14 = (f32[3,128]{1,0:T(4,128)S(1)}, f32[3,128]{1,0:T(4,128)}, u32[]{:S(2)}) copy-start(f32[3,128]{1,0:T(4,128)} %param.25) | copy-start | bytes 4612
  69.7 45.8 %all-to-all-start = ((bf16[32,8,4096]{2,1,0:T(8,128)(2,1)}), bf16[32,8,4096]{2,1,0:T(8,128)(2,1)}, u32[]{:S(2)}, u32[]{:S(2)}) async-start(bf16[32,8,4096]{2,1,0:T(8,128)(2,1)} %get-tuple-element.5), calls=%async_computation | async-start | bytes 4194304 | tf_op jit(solution)/shard_map/all_to_all | solution.py:210
  115.5 39.5 %all-to-all-start.3 = ((bf16[32,16,8,128]{3,2,1,0:T(8,128)(2,1)}), bf16[32,16,8,128]{3,2,1,0:T(8,128)(2,1)S(1)}, u32[]{:S(2)}, u32[]{:S(2)}) async-start(bf16[32,16,8,128]{3,2,1,0:T(8,128)(2,1)} %shard_map.129), calls=%async_computation.3 | async-start | bytes 2097152 | tf_op jit(solution)/shard_map/all_to_all | solution.py:212

commit v2 on v1

v2 whole, which is shorter than its diff:
```python
import functools

import jax
import jax.numpy as jnp
from jax import lax
from jax.experimental import pallas as pl
from jax.experimental.pallas import tpu as pltpu
from jax.sharding import PartitionSpec as P

NORM_GROUPS = 8
NORM_EPS = 1e-5
CHUNKS = 4
BLOCKS = ((2, 1, 8), (1, 2, 4), (2, 1, 2), (1, 2, 2), (2, 1, 2), (1, 1, 2))
MESH = pl.DeviceIdType.MESH
BF16, F32 = jnp.bfloat16, jnp.float32


def peer_step(count):
    step = max(count // 3, 1)
    while any(count % d == 0 and step % d == 0 for d in range(2, count + 1)):
        step += 1
    return step


def patch_shape(stride, bh, bw, first):
    rows = (bh - 1) * stride + 3
    cols = (bw - 1) * stride + 3
    if first:
        cols = bw * stride + 4
    return rows, cols


def encoder_kernel(cfg, x_ref, *refs):
    th, tw, c0, widths, grid_h, grid_w, imgs = cfg
    tiles = grid_h * grid_w
    lanes = tiles * imgs
    w_refs, v_refs = refs[0:6], refs[6:12]
    out_ref = refs[12]
    (xs, send_in, recv_in, send_out, t0, t1, t2, t3, t4, t5, affine, xp, acc_a, y1, z1, y2, z2, y3, s_ref,
     load_sem, in_send, in_recv, in_own, out_send, out_recv, out_own) = refs[13:]
    t_refs = (t0, t1, t2, t3, t4, t5)
    half = th // 2
    width0 = tw * c0
    unit0 = 4 * c0

    my_w, my_h = lax.axis_index("w"), lax.axis_index("h")
    me = my_w * grid_h + my_h
    others = tiles - 1
    step = peer_step(others)

    def peer(n):
        offset = lax.rem(n * step, others) + 1
        pw = lax.rem(my_w + offset // grid_h, grid_w)
        ph = lax.rem(my_h + lax.rem(offset, grid_h), grid_h)
        return pw, ph, pw * grid_h + ph

    def loop(lower, upper, body):
        def step_body(n, carry):
            body(n)
            return carry
        lax.fori_loop(lower, upper, step_body, 0)

    def load(k):
        return pltpu.make_async_copy(x_ref.at[:, :, :, pl.ds(pl.multiple_of(k * lanes, lanes), lanes)], xs.at[k], load_sem.at[k])

    loop(0, CHUNKS, lambda k: load(k).start())
    barrier = pltpu.get_barrier_semaphore()

    def greet(n):
        pw, ph, _ = peer(n)
        pl.semaphore_signal(barrier, inc=1, device_id={"w": pw, "h": ph}, device_id_type=MESH)

    loop(0, others, greet)

    def iota(shape, dim):
        return lax.broadcasted_iota(jnp.int32, shape, dim)

    both = 2 * lanes
    o, i = iota((both, both), 0), iota((both, both), 1)
    o_tile, o_half, o_img = o // (2 * imgs), (o // imgs) % 2, o % imgs
    pair = jnp.where(i == o_half * lanes + o_tile * imgs + o_img, 1.0, 0.0).astype(BF16)

    def pack(k):
        load(k).wait()
        for r in range(half):
            cat = jnp.concatenate([xs[k, r].reshape(width0, lanes), xs[k, r + half].reshape(width0, lanes)], axis=1)
            res = lax.dot_general(pair, cat, (((1,), (1,)), ((), ())), preferred_element_type=F32)
            send_in[k, :, :, r * width0:(r + 1) * width0] = res.reshape(tiles, 2 * imgs, width0).astype(BF16)

    def copy_in(k, n):
        pw, ph, p = peer(n)
        return pltpu.make_async_remote_copy(
            src_ref=send_in.at[k, p], dst_ref=recv_in.at[k, me], send_sem=in_send.at[k, n], recv_sem=in_recv.at[k, n],
            device_id={"w": pw, "h": ph}, device_id_type=MESH)

    def own_in(k):
        return pltpu.make_async_copy(send_in.at[k, me], recv_in.at[k, me], in_own.at[k])

    def copy_out(k, n):
        pw, ph, p = peer(n)
        return pltpu.make_async_remote_copy(
            src_ref=send_out.at[k, p], dst_ref=out_ref.at[k, me], send_sem=out_send.at[k, n], recv_sem=out_recv.at[k, n],
            device_id={"w": pw, "h": ph}, device_id_type=MESH)

    def own_out(k):
        return pltpu.make_async_copy(send_out.at[k, me], out_ref.at[k, me], out_own.at[k])

    def start(k, copy, own):
        loop(0, others, lambda n: copy(k, n).start())
        own(k).start()

    def wait(k, copy, own):
        loop(0, others, lambda n: copy(k, n).wait())
        own(k).wait()

    pack(0)
    pl.semaphore_wait(barrier, others)
    start(0, copy_in, own_in)

    def pack_body(k):
        pack(k)
        start(k, copy_in, own_in)

    loop(1, CHUNKS, pack_body)

    for layer, (stride, bh, bw) in enumerate(BLOCKS):
        w_ref = w_refs[layer]
        ci, co = w_ref.shape[2], w_ref.shape[3]
        rows, cols = patch_shape(stride, bh, bw, layer == 0)
        off = 3 if layer == 0 else 0
        bands = [jnp.concatenate([w_ref[dy, dx].astype(F32) for dx in range(3)], axis=0).T for dy in range(3)]
        for bi in range(bh):
            for bj in range(bw):
                parts, at = [], 0
                for dy in range(3):
                    begin = ((stride * bi + dy) * cols + off + stride * bj) * ci
                    if begin > at:
                        parts.append(jnp.zeros((co, begin - at), F32))
                    parts.append(bands[dy])
                    at = begin + 3 * ci
                if rows * cols * ci > at:
                    parts.append(jnp.zeros((co, rows * cols * ci - at), F32))
                t_refs[layer][(bi * bw + bj) * co:(bi * bw + bj + 1) * co] = jnp.concatenate(parts, axis=1).astype(BF16)
        for q in range(3):
            affine[layer, q, 0:co] = jnp.broadcast_to(v_refs[layer][q:q + 1], (lanes, co)).T

    src_l, dst_l = iota((lanes, lanes), 0), iota((lanes, lanes), 1)

    def perm(dh, dw):
        t = dst_l // imgs
        h, w = t % grid_h + dh, t // grid_h + dw
        inside = (h >= 0) & (h < grid_h) & (w >= 0) & (w < grid_w)
        want = (w * grid_h + h) * imgs + dst_l % imgs
        return jnp.where(inside & (src_l == want), 1.0, 0.0).astype(BF16)

    above, below, left, right = perm(-1, 0), perm(1, 0), perm(0, -1), perm(0, 1)
    same_image = jnp.where(src_l % imgs == dst_l % imgs, 1.0, 0.0)

    def move(value, matrix):
        return jnp.dot(value, matrix, preferred_element_type=F32).astype(BF16)

    def halos(buf, rows, cols, unit, both_sides):
        buf[0] = move(buf[rows], above)
        if both_sides:
            buf[rows + 1] = move(buf[1], below)
        for r in range(rows + (2 if both_sides else 1)):
            buf[r, 0:unit] = move(buf[r, cols * unit:(cols + 1) * unit], left)
            if both_sides:
                buf[r, (cols + 1) * unit:(cols + 2) * unit] = move(buf[r, unit:2 * unit], right)

    def conv(buf, w_ref, stride, bh, bw, ci, co, out_h, out_w, first):
        rows, cols = patch_shape(stride, bh, bw, first)
        s_ref[:, 0:co] = jnp.zeros((2, co, lanes), F32)
        far = out_h // 2

        def row_body(n, carry):
            for j in range(out_w // bw):
                start = j * bw * stride * ci
                patches = []
                for base in (n * bh, n * bh + far):
                    patches.append(jnp.concatenate([buf[base * stride + r, start:start + cols * ci] for r in range(rows)], axis=0))
                res = jnp.dot(w_ref[...], jnp.concatenate(patches, axis=1), preferred_element_type=F32)
                parts = [res[p * co:(p + 1) * co, q * lanes:(q + 1) * lanes] for p in range(bh * bw) for q in range(2)]
                s_ref[0, 0:co] += functools.reduce(jnp.add, parts)
                s_ref[1, 0:co] += functools.reduce(jnp.add, [p * p for p in parts])
                for b in range(bh):
                    for q in range(2):
                        acc_a[n * bh + b + q * far, j * bw * co:(j + 1) * bw * co] = res[b * bw * co:(b + 1) * bw * co, q * lanes:(q + 1) * lanes]
            return carry

        lax.fori_loop(0, far // bh, row_body, 0)

    def stats(layer, co, pixels):
        per = co // NORM_GROUPS
        group = jnp.where(iota((co, co), 0) // per == iota((co, co), 1) // per, 1.0, 0.0)
        hi = lax.Precision.HIGHEST
        tot = jnp.dot(s_ref[:, 0:co].reshape(2 * co, lanes), same_image, precision=hi, preferred_element_type=F32) / pixels
        mean_c, sq_c = tot[0:co], tot[co:2 * co]
        var_c = jnp.maximum(sq_c - mean_c * mean_c, 0.0)
        bias, gain, shift = affine[layer, 0, 0:co], affine[layer, 1, 0:co], affine[layer, 2, 0:co]
        mean_a = mean_c + bias
        m = jnp.dot(group, mean_a, precision=hi, preferred_element_type=F32) / per
        dev = mean_a - m
        q = jnp.dot(group, var_c + dev * dev, precision=hi, preferred_element_type=F32) / per
        scale = lax.rsqrt(q + NORM_EPS) * gain
        return scale, shift + (bias - m) * scale

    def normalise(scale, offset, co, out_h, out_w, dst_buf):
        def row_body(r, carry):
            for j in range(out_w):
                val = acc_a[r, j * co:(j + 1) * co]
                dst_buf[r + 1, (j + 1) * co:(j + 2) * co] = jnp.maximum(val * scale + offset, 0.0).astype(BF16)
            return carry

        lax.fori_loop(0, out_h, row_body, 0)

    bufs = (xp, y1, z1, y2, z2, y3)

    def chunk(k):
        wait(k, copy_in, own_in)
        for r in range(half):
            block = recv_in[k, :, :, r * width0:(r + 1) * width0].astype(F32).reshape(both, width0)
            res = jnp.dot(block.T.astype(BF16), pair, preferred_element_type=F32).astype(BF16)
            xp[r + 1, unit0:unit0 + width0] = res[:, 0:lanes]
            xp[r + 1 + half, unit0:unit0 + width0] = res[:, lanes:both]
        xp[0, unit0:unit0 + width0] = move(xp[th, unit0:unit0 + width0], above)
        for r in range(th + 1):
            xp[r, 0:unit0] = move(xp[r, width0:width0 + unit0], left)

        h, w, ci = th, tw, c0
        for layer in range(6):
            stride, bh, bw = BLOCKS[layer]
            co = widths[layer // 2]
            h, w = h // stride, w // stride
            conv(bufs[layer], t_refs[layer], stride, bh, bw, ci, co, h, w, layer == 0)
            scale, offset = stats(layer, co, float(h * w * tiles))
            ci = co
            if layer < 5:
                normalise(scale, offset, co, h, w, bufs[layer + 1])
                halos(bufs[layer + 1], h, w, co, layer % 2 == 0)

        def finish(p):
            r, j = p // w, p % w
            return jnp.maximum(acc_a[r, j * ci:(j + 1) * ci] * scale + offset, 0.0).astype(BF16)

        for p in range(h * w // 2):
            cat = jnp.concatenate([finish(p), finish(p + h * w // 2)], axis=1)
            res = lax.dot_general(pair, cat, (((1,), (1,)), ((), ())), preferred_element_type=F32)
            send_out[k, :, p] = res.reshape(tiles, 2 * imgs, ci).astype(BF16)
        start(k, copy_out, own_out)

    loop(0, CHUNKS, chunk)
    loop(0, CHUNKS, lambda k: wait(k, copy_out, own_out))


def encode(cfg, x, kernels, affines):
    th, tw, c0, widths, grid_h, grid_w, imgs = cfg
    tiles = grid_h * grid_w
    lanes = tiles * imgs
    c1, c2, c3 = widths
    vmem = pl.BlockSpec(memory_space=pltpu.VMEM)
    hbm = pl.BlockSpec(memory_space=pl.ANY)
    h1, w1, h2, w2, h3, w3 = th // 2, tw // 2, th // 4, tw // 4, th // 8, tw // 8
    tables = []
    for layer, (stride, bh, bw) in enumerate(BLOCKS):
        rows, cols = patch_shape(stride, bh, bw, layer == 0)
        tables.append(pltpu.VMEM((bh * bw * kernels[layer].shape[3], rows * cols * kernels[layer].shape[2]), BF16))
    dma = pltpu.SemaphoreType.DMA
    return pl.pallas_call(
        functools.partial(encoder_kernel, cfg),
        out_shape=jax.ShapeDtypeStruct((CHUNKS, tiles, h3 * w3 // 2, 2 * imgs, c3), BF16),
        in_specs=[hbm] + [vmem] * 12,
        out_specs=hbm,
        scratch_shapes=[
            pltpu.VMEM((CHUNKS, th, tw, c0, lanes), BF16),
            pltpu.VMEM((CHUNKS, tiles, 2 * imgs, th * tw * c0 // 2), BF16),
            pltpu.VMEM((CHUNKS, tiles, 2 * imgs, th * tw * c0 // 2), BF16),
            pltpu.VMEM((CHUNKS, tiles, h3 * w3 // 2, 2 * imgs, c3), BF16),
            *tables,
            pltpu.VMEM((6, 3, c3, lanes), F32),
            pltpu.VMEM((th + 1, (tw + 4) * c0, lanes), BF16),
            pltpu.VMEM((h1, w1 * c1, lanes), F32),
            pltpu.VMEM((h1 + 2, (w1 + 2) * c1, lanes), BF16),
            pltpu.VMEM((h1 + 1, (w1 + 1) * c1, lanes), BF16),
            pltpu.VMEM((h2 + 2, (w2 + 2) * c2, lanes), BF16),
            pltpu.VMEM((h2 + 1, (w2 + 1) * c2, lanes), BF16),
            pltpu.VMEM((h3 + 2, (w3 + 2) * c3, lanes), BF16),
            pltpu.VMEM((2, c3, lanes), F32),
            dma((CHUNKS,)),
            dma((CHUNKS, tiles - 1)), dma((CHUNKS, tiles - 1)), dma((CHUNKS,)),
            dma((CHUNKS, tiles - 1)), dma((CHUNKS, tiles - 1)), dma((CHUNKS,)),
        ],
        compiler_params=pltpu.CompilerParams(vmem_limit_bytes=63 * 1024 * 1024, collective_id=0, has_side_effects=True),
    )(x, *kernels, *affines)


def solution(mesh):
    grid_h = mesh.shape["h"]
    grid_w = mesh.shape["w"]
    tiles = grid_h * grid_w
    act_spec = P("batch", "h", "w")

    def local_forward(tile, *params):
        count, th, tw, c0 = tile.shape
        kernels, affines = params[0::2], params[1::2]
        widths = tuple(kernels[2 * s].shape[3] for s in range(3))
        cfg = (th, tw, c0, widths, grid_h, grid_w, count // tiles // CHUNKS)
        res = encode(cfg, tile.transpose(1, 2, 3, 0), kernels, affines)
        imgs = count // tiles // CHUNKS
        res = res.reshape(CHUNKS, tiles, -1, 2, imgs, widths[2])
        return res.transpose(0, 1, 4, 3, 2, 5).reshape(count, th // 8, tw // 8, widths[2])

    return jax.shard_map(local_forward, mesh=mesh, in_specs=(act_spec,) + (P(),) * 12, out_specs=act_spec, check_vma=False)
```

time: 182 us -> 116 us (0.64); the launches traced: 180 us -> 116 us
  local copies, waits for them, and re-layouts: 56 us -> 3.53 us
  Pallas kernels: 73.7 us -> 113 us
  blocking collectives: 22.9 us -> 0 us
  starting transfers between devices: 21.8 us -> 0 us
  other arithmetic: 5.41 us -> 0 us
    pallas_call x2 -> x1, Pallas kernels: 66.4 us -> 113 us  [encode(): pl.pallas_call(functools.partial(encoder_kernel, cfg), out_shape=jax.Shap...]
    reshape x26 -> x0, local copies, waits for them, and re-layouts: 23.7 us -> none  [block_weights(): parts.append(padded.reshape(kernel.shape[3], -1))]
    all_to_all x1 -> x0, blocking collectives: 22.9 us -> none  [local_forward(): outs.append(lax.all_to_all(res, ('w', 'h'), 0, 0))]
    all_to_all x3 -> x0, starting transfers between devices: 21.8 us -> none  [the longest x2 15.5 us: local_forward(): got = lax.all_to_all(rows[k], ('w', 'h'), 0, 0)]
    unnamed x50 -> x0, local copies, waits for them, and re-layouts: 18.4 us -> none
    pallas_call x1 -> x0, Pallas kernels: 7.28 us -> none  [pack(): pl.pallas_call(pack_kernel, grid=(th // 2,), out_shape=jax.ShapeDtypeStru...]
    pad x6 -> x0, local copies, waits for them, and re-layouts: 5.79 us -> none  [block_weights(): jnp.pad(flipped, ((0, 0), (top, rows - 3 - top), (left, cols - 3 - left),...]
    concatenate x4 -> x0, other arithmetic: 5.22 us -> none  [block_weights(): return jnp.concatenate(parts, axis=0)]
  transfers between devices with their start and end apart: 3 -> 0, of which waited for: 0 -> 0; matrix products, arithmetic and copies ran while one was open for 30% -> 0% of each run, Pallas kernels for 37% -> 0%
where the time goes in v2:
time: 116 us
  Pallas kernels  113 us (97%)
  local copies, waits for them, and re-layouts  3.53 us (3%)
    pallas_call x1, Pallas kernels, encode(): pl.pallas_call(functools.partial(encoder_kernel, cfg), out_shape=jax.Shap...  113 us
    transpose x1, local copies, waits for them, and re-layouts, local_forward(): res.transpose(0, 1, 4, 3, 2, 5).reshape(count, th // 8, tw // 8, widths[2])  3.53 us

profile of v2, /device:TPU:97, one launch (start us, length us, event | category | flops | bytes accessed | tf_op | source)
XLA Modules:
  0.0 116.1 jit_solution(16922843748919425161)
XLA Ops:
  0.0 112.6 %shard_map.127 = bf16[4,32,8,8,128]{4,3,2,1,0:T(8,128)(2,1)} custom-call(bf16[16,64,4,512]{3,2,1,0:T(4,128)(2,1)} %bitcast.6, bf16[3,3,4,32]{3,2,1,0:T(4,128)(2,1)} %refs_0_.1, bf16[3,3,32,32]{3,2,1,0:T(8,128)(2,1)} %refs_1_.1, bf16[3,3,32,64]{3,2,1,0:T(8,128)(2,1)} %refs_2_.1, bf16[3,3,64,64]{3,2,1,0:T(8,128)(2,1)} %refs_3_.1, ...), custom_call_target="tpu_custom_call" | custom-call | tf_op jit(solution)/shard_map/pallas_call | solution.py:269
  112.6 3.5 %copy.14 = bf16[4,32,4,2,8,128]{5,4,3,2,1,0:T(8,128)(2,1)} copy(bf16[4,32,4,2,8,128]{5,2,3,4,1,0:T(4,128)(2,1)} %bitcast.5) | data formatting | bytes 4194304 | tf_op jit(solution)/shard_map/transpose | solution.py:311

commit v3 on v2

--- a/solution.py
+++ b/solution.py
@@ -106,7 +106,8 @@
         return pltpu.make_async_copy(send_out.at[k, me], out_ref.at[k, me], out_own.at[k])
 
     def start(k, copy, own):
-        loop(0, others, lambda n: copy(k, n).start())
+        for n in range(others):
+            copy(k, n).start()
         own(k).start()
 
     def wait(k, copy, own):
@@ -145,28 +146,36 @@
             affine[layer, q, 0:co] = jnp.broadcast_to(v_refs[layer][q:q + 1], (lanes, co)).T
 
     src_l, dst_l = iota((lanes, lanes), 0), iota((lanes, lanes), 1)
-
-    def perm(dh, dw):
-        t = dst_l // imgs
-        h, w = t % grid_h + dh, t // grid_h + dw
+    same_image = jnp.where(src_l % imgs == dst_l % imgs, 1.0, 0.0).astype(BF16)
+    lane = iota((16, lanes), 1)
+    lane_h, lane_w = (lane // imgs) % grid_h, lane // (imgs * grid_h)
+
+    def mask(dh, dw):
+        h, w = lane_h + dh, lane_w + dw
         inside = (h >= 0) & (h < grid_h) & (w >= 0) & (w < grid_w)
-        want = (w * grid_h + h) * imgs + dst_l % imgs
-        return jnp.where(inside & (src_l == want), 1.0, 0.0).astype(BF16)
-
-    above, below, left, right = perm(-1, 0), perm(1, 0), perm(0, -1), perm(0, 1)
-    same_image = jnp.where(src_l % imgs == dst_l % imgs, 1.0, 0.0)
-
-    def move(value, matrix):
-        return jnp.dot(value, matrix, preferred_element_type=F32).astype(BF16)
+        return jnp.where(inside, 1.0, 0.0).astype(BF16)
+
+    masks = {(dh, dw): mask(dh, dw) for dh in (-1, 0, 1) for dw in (-1, 0, 1) if (dh, dw) != (0, 0)}
+
+    def take(value, dh, dw):
+        shift = (-(dh + dw * grid_h) * imgs) % lanes
+        moved = pltpu.roll(value, shift, 1).reshape(-1, 16, lanes)
+        return (moved * masks[(dh, dw)][None]).reshape(value.shape)
 
     def halos(buf, rows, cols, unit, both_sides):
-        buf[0] = move(buf[rows], above)
-        if both_sides:
-            buf[rows + 1] = move(buf[1], below)
-        for r in range(rows + (2 if both_sides else 1)):
-            buf[r, 0:unit] = move(buf[r, cols * unit:(cols + 1) * unit], left)
-            if both_sides:
-                buf[r, (cols + 1) * unit:(cols + 2) * unit] = move(buf[r, unit:2 * unit], right)
+        sides = (-1, 0, 1) if both_sides else (-1, 0)
+        for dh in sides:
+            for dw in sides:
+                if (dh, dw) == (0, 0):
+                    continue
+                src_r = {-1: (rows, rows + 1), 0: (1, rows + 1), 1: (1, 2)}[dh]
+                dst_r = {-1: 0, 0: 1, 1: rows + 1}[dh]
+                src_c = {-1: (cols, cols + 1), 0: (1, cols + 1), 1: (1, 2)}[dw]
+                dst_c = {-1: 0, 0: 1, 1: cols + 1}[dw]
+                span = (src_c[1] - src_c[0]) * unit
+                for n in range(src_r[1] - src_r[0]):
+                    value = buf[src_r[0] + n, src_c[0] * unit:src_c[1] * unit]
+                    buf[dst_r + n, dst_c * unit:dst_c * unit + span] = take(value, dh, dw)
 
     def conv(buf, w_ref, stride, bh, bw, ci, co, out_h, out_w, first):
         rows, cols = patch_shape(stride, bh, bw, first)
@@ -190,18 +199,32 @@
 
         lax.fori_loop(0, far // bh, row_body, 0)
 
+    def group_sum(x, co):
+        per = co // NORM_GROUPS
+        span = max(per, 8)
+        y = x.reshape(co // span, span, lanes)
+        if per >= 8:
+            return jnp.broadcast_to(jnp.sum(y, axis=1, keepdims=True), y.shape).reshape(co, lanes)
+        row = iota((1, span, lanes), 1) // per
+        res = jnp.zeros_like(y)
+        for g in range(span // per):
+            part = jnp.sum(jnp.where(row == g, y, 0.0), axis=1, keepdims=True)
+            res = jnp.where(row == g, part, res)
+        return res.reshape(co, lanes)
+
     def stats(layer, co, pixels):
-        per = co // NORM_GROUPS
-        group = jnp.where(iota((co, co), 0) // per == iota((co, co), 1) // per, 1.0, 0.0)
-        hi = lax.Precision.HIGHEST
-        tot = jnp.dot(s_ref[:, 0:co].reshape(2 * co, lanes), same_image, precision=hi, preferred_element_type=F32) / pixels
-        mean_c, sq_c = tot[0:co], tot[co:2 * co]
-        var_c = jnp.maximum(sq_c - mean_c * mean_c, 0.0)
         bias, gain, shift = affine[layer, 0, 0:co], affine[layer, 1, 0:co], affine[layer, 2, 0:co]
-        mean_a = mean_c + bias
-        m = jnp.dot(group, mean_a, precision=hi, preferred_element_type=F32) / per
-        dev = mean_a - m
-        q = jnp.dot(group, var_c + dev * dev, precision=hi, preferred_element_type=F32) / per
+        s1, s2 = s_ref[0, 0:co], s_ref[1, 0:co]
+        with_bias = pixels * bias
+        part = jnp.concatenate([group_sum(s1 + with_bias, co), group_sum(s2 + bias * (2.0 * s1 + with_bias), co)], axis=0)
+        p0 = part.astype(BF16)
+        rest = part - p0.astype(F32)
+        p1 = rest.astype(BF16)
+        p2 = (rest - p1.astype(F32)).astype(BF16)
+        tot = jnp.dot(jnp.concatenate([p0, p1, p2], axis=0), same_image, preferred_element_type=F32)
+        tot = (tot[0:2 * co] + tot[2 * co:4 * co] + tot[4 * co:6 * co]) * (1.0 / (pixels * tiles * (co // NORM_GROUPS)))
+        m = tot[0:co]
+        q = jnp.maximum(tot[co:2 * co] - m * m, 0.0)
         scale = lax.rsqrt(q + NORM_EPS) * gain
         return scale, shift + (bias - m) * scale
 
@@ -223,9 +246,10 @@
             res = jnp.dot(block.T.astype(BF16), pair, preferred_element_type=F32).astype(BF16)
             xp[r + 1, unit0:unit0 + width0] = res[:, 0:lanes]
             xp[r + 1 + half, unit0:unit0 + width0] = res[:, lanes:both]
-        xp[0, unit0:unit0 + width0] = move(xp[th, unit0:unit0 + width0], above)
-        for r in range(th + 1):
-            xp[r, 0:unit0] = move(xp[r, width0:width0 + unit0], left)
+        xp[0, unit0:unit0 + width0] = take(xp[th, unit0:unit0 + width0], -1, 0)
+        xp[0, 0:unit0] = take(xp[th, width0:width0 + unit0], -1, -1)
+        for r in range(1, th + 1):
+            xp[r, 0:unit0] = take(xp[r, width0:width0 + unit0], 0, -1)
 
         h, w, ci = th, tw, c0
         for layer in range(6):
@@ -233,7 +257,7 @@
             co = widths[layer // 2]
             h, w = h // stride, w // stride
             conv(bufs[layer], t_refs[layer], stride, bh, bw, ci, co, h, w, layer == 0)
-            scale, offset = stats(layer, co, float(h * w * tiles))
+            scale, offset = stats(layer, co, float(h * w))
             ci = co
             if layer < 5:
                 normalise(scale, offset, co, h, w, bufs[layer + 1])

time: 116 us -> 105 us (0.905); the launches traced: 116 us -> 103 us
  Pallas kernels: 113 us -> 99.8 us
    pallas_call x1, Pallas kernels: 113 us -> 99.8 us  [encode(): pl.pallas_call(functools.partial(encoder_kernel, cfg), out_shape=jax.Shap...]
where the time goes in v3:
time: 105 us; the launch traced here: 103 us
  Pallas kernels  99.8 us (95%)
  local copies, waits for them, and re-layouts  3.53 us (3%)
    pallas_call x1, Pallas kernels, encode(): pl.pallas_call(functools.partial(encoder_kernel, cfg), out_shape=jax.Shap...  99.8 us
    transpose x1, local copies, waits for them, and re-layouts, local_forward(): res.transpose(0, 1, 4, 3, 2, 5).reshape(count, th // 8, tw // 8, widths[2])  3.53 us

profile of v3, /device:TPU:97, one launch (start us, length us, event | category | flops | bytes accessed | tf_op | source)
XLA Modules:
  0.0 103.3 jit_solution(10268070726479861282)
XLA Ops:
  0.0 99.8 %shard_map.127 = bf16[4,32,8,8,128]{4,3,2,1,0:T(8,128)(2,1)} custom-call(bf16[16,64,4,512]{3,2,1,0:T(4,128)(2,1)} %bitcast.6, bf16[3,3,4,32]{3,2,1,0:T(4,128)(2,1)} %refs_0_.1, bf16[3,3,32,32]{3,2,1,0:T(8,128)(2,1)} %refs_1_.1, bf16[3,3,32,64]{3,2,1,0:T(8,128)(2,1)} %refs_2_.1, bf16[3,3,64,64]{3,2,1,0:T(8,128)(2,1)} %refs_3_.1, ...), custom_call_target="tpu_custom_call" | custom-call | tf_op jit(solution)/shard_map/pallas_call | solution.py:293
  99.8 3.5 %copy.14 = bf16[4,32,4,2,8,128]{5,4,3,2,1,0:T(8,128)(2,1)} copy(bf16[4,32,4,2,8,128]{5,2,3,4,1,0:T(4,128)(2,1)} %bitcast.5) | data formatting | bytes 4194304 | tf_op jit(solution)/shard_map/transpose | solution.py:335

commit v4 on v3

--- a/solution.py
+++ b/solution.py
@@ -15,11 +15,15 @@
 BF16, F32 = jnp.bfloat16, jnp.float32
 
 
-def peer_step(count):
-    step = max(count // 3, 1)
-    while any(count % d == 0 and step % d == 0 for d in range(2, count + 1)):
-        step += 1
-    return step
+def send_order(grid_w, grid_h):
+    def ring(d, size):
+        return min(d, size - d)
+
+    def hops(n):
+        dw, dh = n // grid_h, n % grid_h
+        return ring(dw, grid_w) + ring(dh // 2, grid_h // 2)
+
+    return sorted(range(1, grid_w * grid_h), key=lambda n: -hops(n))
 
 
 def patch_shape(stride, bh, bw, first):
@@ -34,10 +38,13 @@
     th, tw, c0, widths, grid_h, grid_w, imgs = cfg
     tiles = grid_h * grid_w
     lanes = tiles * imgs
-    w_refs, v_refs = refs[0:6], refs[6:12]
+    param_refs = refs[0:12]
     out_ref = refs[12]
-    (xs, send_in, recv_in, send_out, t0, t1, t2, t3, t4, t5, affine, xp, acc_a, y1, z1, y2, z2, y3, s_ref,
-     load_sem, in_send, in_recv, in_own, out_send, out_recv, out_own) = refs[13:]
+    (xs, send_in, recv_in, send_out, t0, t1, t2, t3, t4, t5, *rest) = refs[13:]
+    param_bufs = rest[0:12]
+    (affine, xp, acc_a, y1, z1, y2, z2, y3, s_ref,
+     load_sem, param_sem, in_send, in_recv, in_own, out_send, out_recv, out_own) = rest[12:]
+    w_refs, v_refs = param_bufs[0:6], param_bufs[6:12]
     t_refs = (t0, t1, t2, t3, t4, t5)
     half = th // 2
     width0 = tw * c0
@@ -46,10 +53,9 @@
     my_w, my_h = lax.axis_index("w"), lax.axis_index("h")
     me = my_w * grid_h + my_h
     others = tiles - 1
-    step = peer_step(others)
 
     def peer(n):
-        offset = lax.rem(n * step, others) + 1
+        offset = n + 1
         pw = lax.rem(my_w + offset // grid_h, grid_w)
         ph = lax.rem(my_h + lax.rem(offset, grid_h), grid_h)
         return pw, ph, pw * grid_h + ph
@@ -64,6 +70,9 @@
         return pltpu.make_async_copy(x_ref.at[:, :, :, pl.ds(pl.multiple_of(k * lanes, lanes), lanes)], xs.at[k], load_sem.at[k])
 
     loop(0, CHUNKS, lambda k: load(k).start())
+    params = [pltpu.make_async_copy(param_refs[n], param_bufs[n], param_sem.at[n]) for n in range(12)]
+    for param in params:
+        param.start()
     barrier = pltpu.get_barrier_semaphore()
 
     def greet(n):
@@ -106,8 +115,8 @@
         return pltpu.make_async_copy(send_out.at[k, me], out_ref.at[k, me], out_own.at[k])
 
     def start(k, copy, own):
-        for n in range(others):
-            copy(k, n).start()
+        for offset in send_order(grid_w, grid_h):
+            copy(k, offset - 1).start()
         own(k).start()
 
     def wait(k, copy, own):
@@ -124,6 +133,8 @@
 
     loop(1, CHUNKS, pack_body)
 
+    for param in params:
+        param.wait()
     for layer, (stride, bh, bw) in enumerate(BLOCKS):
         w_ref = w_refs[layer]
         ci, co = w_ref.shape[2], w_ref.shape[3]
@@ -282,8 +293,6 @@
     tiles = grid_h * grid_w
     lanes = tiles * imgs
     c1, c2, c3 = widths
-    vmem = pl.BlockSpec(memory_space=pltpu.VMEM)
-    hbm = pl.BlockSpec(memory_space=pl.ANY)
     h1, w1, h2, w2, h3, w3 = th // 2, tw // 2, th // 4, tw // 4, th // 8, tw // 8
     tables = []
     for layer, (stride, bh, bw) in enumerate(BLOCKS):
@@ -293,14 +302,15 @@
     return pl.pallas_call(
         functools.partial(encoder_kernel, cfg),
         out_shape=jax.ShapeDtypeStruct((CHUNKS, tiles, h3 * w3 // 2, 2 * imgs, c3), BF16),
-        in_specs=[hbm] + [vmem] * 12,
-        out_specs=hbm,
+        in_specs=[pl.BlockSpec(memory_space=pltpu.HBM)] * 13,
+        out_specs=pl.BlockSpec(memory_space=pl.ANY),
         scratch_shapes=[
             pltpu.VMEM((CHUNKS, th, tw, c0, lanes), BF16),
             pltpu.VMEM((CHUNKS, tiles, 2 * imgs, th * tw * c0 // 2), BF16),
             pltpu.VMEM((CHUNKS, tiles, 2 * imgs, th * tw * c0 // 2), BF16),
             pltpu.VMEM((CHUNKS, tiles, h3 * w3 // 2, 2 * imgs, c3), BF16),
             *tables,
+            *[pltpu.VMEM(p.shape, p.dtype) for p in (*kernels, *affines)],
             pltpu.VMEM((6, 3, c3, lanes), F32),
             pltpu.VMEM((th + 1, (tw + 4) * c0, lanes), BF16),
             pltpu.VMEM((h1, w1 * c1, lanes), F32),
@@ -310,12 +320,12 @@
             pltpu.VMEM((h2 + 1, (w2 + 1) * c2, lanes), BF16),
             pltpu.VMEM((h3 + 2, (w3 + 2) * c3, lanes), BF16),
             pltpu.VMEM((2, c3, lanes), F32),
-            dma((CHUNKS,)),
+            dma((CHUNKS,)), dma((12,)),
             dma((CHUNKS, tiles - 1)), dma((CHUNKS, tiles - 1)), dma((CHUNKS,)),
             dma((CHUNKS, tiles - 1)), dma((CHUNKS, tiles - 1)), dma((CHUNKS,)),
         ],
-        compiler_params=pltpu.CompilerParams(vmem_limit_bytes=63 * 1024 * 1024, collective_id=0, has_side_effects=True),
-    )(x, *kernels, *affines)
+        compiler_params=pltpu.CompilerParams(vmem_limit_bytes=40 * 1024 * 1024, collective_id=0, has_side_effects=True),
+    )(*[pltpu.with_memory_space_constraint(p, pltpu.HBM) for p in (x, *kernels, *affines)])
 
 
 def solution(mesh):

time: 105 us -> 95.7 us (0.911); the launches traced: 103 us -> 95.6 us
  Pallas kernels: 99.8 us -> 93.7 us
  local copies, waits for them, and re-layouts: 3.53 us -> 1.94 us
    pallas_call x1, Pallas kernels: 99.8 us -> 93.7 us  [encode(): pl.pallas_call(functools.partial(encoder_kernel, cfg), out_shape=jax.Shap...]
    transpose x1, local copies, waits for them, and re-layouts: 3.53 us -> 1.94 us  [local_forward(): res.transpose(0, 1, 4, 3, 2, 5).reshape(count, th // 8, tw // 8, widths[2])]
where the time goes in v4:
time: 95.7 us; the launch traced here: 95.6 us
  Pallas kernels  93.7 us (98%)
  local copies, waits for them, and re-layouts  1.94 us (2%)
    pallas_call x1, Pallas kernels, encode(): pl.pallas_call(functools.partial(encoder_kernel, cfg), out_shape=jax.Shap...  93.7 us
    transpose x1, local copies, waits for them, and re-layouts, local_forward(): res.transpose(0, 1, 4, 3, 2, 5).reshape(count, th // 8, tw // 8, widths[2])  1.94 us

profile of v4, /device:TPU:97, one launch (start us, length us, event | category | flops | bytes accessed | tf_op | source)
XLA Modules:
  0.0 95.6 jit_solution(5647782072886039517)
XLA Ops:
  0.0 93.7 %shard_map.127 = bf16[4,32,8,8,128]{4,3,2,1,0:T(8,128)(2,1)S(1)} custom-call(bf16[16,64,4,512]{3,2,1,0:T(4,128)(2,1)} %bitcast.6, bf16[3,3,4,32]{3,2,1,0:T(4,128)(2,1)} %refs_0_.1, bf16[3,3,32,32]{3,2,1,0:T(8,128)(2,1)} %refs_1_.1, bf16[3,3,32,64]{3,2,1,0:T(8,128)(2,1)} %refs_2_.1, bf16[3,3,64,64]{3,2,1,0:T(8,128)(2,1)} %refs_3_.1, ...), custom_call_target="tpu_custom_call" | custom-call | tf_op jit(solution)/shard_map/pallas_call | solution.py:302
  93.7 1.9 %copy.14 = bf16[4,32,4,2,8,128]{5,4,3,2,1,0:T(8,128)(2,1)} copy(bf16[4,32,4,2,8,128]{5,2,3,4,1,0:T(4,128)(2,1)S(1)} %bitcast.5) | data formatting | bytes 4194304 | tf_op jit(solution)/shard_map/transpose | solution.py:345

commit v5 on v4

--- a/solution.py
+++ b/solution.py
@@ -1,4 +1,5 @@
 import functools
+import random
 
 import jax
 import jax.numpy as jnp
@@ -10,20 +11,16 @@
 NORM_GROUPS = 8
 NORM_EPS = 1e-5
 CHUNKS = 4
+SEED = 12
 BLOCKS = ((2, 1, 8), (1, 2, 4), (2, 1, 2), (1, 2, 2), (2, 1, 2), (1, 1, 2))
 MESH = pl.DeviceIdType.MESH
 BF16, F32 = jnp.bfloat16, jnp.float32
 
 
 def send_order(grid_w, grid_h):
-    def ring(d, size):
-        return min(d, size - d)
-
-    def hops(n):
-        dw, dh = n // grid_h, n % grid_h
-        return ring(dw, grid_w) + ring(dh // 2, grid_h // 2)
-
-    return sorted(range(1, grid_w * grid_h), key=lambda n: -hops(n))
+    order = list(range(1, grid_w * grid_h))
+    random.Random(SEED).shuffle(order)
+    return order
 
 
 def patch_shape(stride, bh, bw, first):
@@ -43,7 +40,7 @@
     (xs, send_in, recv_in, send_out, t0, t1, t2, t3, t4, t5, *rest) = refs[13:]
     param_bufs = rest[0:12]
     (affine, xp, acc_a, y1, z1, y2, z2, y3, s_ref,
-     load_sem, param_sem, in_send, in_recv, in_own, out_send, out_recv, out_own) = rest[12:]
+     row_sem, load_sem, param_sem, in_send, in_recv, in_own, out_send, out_recv, out_own) = rest[12:]
     w_refs, v_refs = param_bufs[0:6], param_bufs[6:12]
     t_refs = (t0, t1, t2, t3, t4, t5)
     half = th // 2
@@ -69,17 +66,23 @@
     def load(k):
         return pltpu.make_async_copy(x_ref.at[:, :, :, pl.ds(pl.multiple_of(k * lanes, lanes), lanes)], xs.at[k], load_sem.at[k])
 
+    barrier = pltpu.get_barrier_semaphore()
+    in_column = [dw * grid_h for dw in range(1, grid_w)]
+    near = in_column + list(range(1, grid_h))
+
+    def greet(semaphore, offset):
+        pw, ph, _ = peer(offset - 1)
+        pl.semaphore_signal(semaphore, inc=1, device_id={"w": pw, "h": ph}, device_id_type=MESH)
+
+    for offset in near:
+        greet(barrier, offset)
     loop(0, CHUNKS, lambda k: load(k).start())
     params = [pltpu.make_async_copy(param_refs[n], param_bufs[n], param_sem.at[n]) for n in range(12)]
     for param in params:
         param.start()
-    barrier = pltpu.get_barrier_semaphore()
-
-    def greet(n):
-        pw, ph, _ = peer(n)
-        pl.semaphore_signal(barrier, inc=1, device_id={"w": pw, "h": ph}, device_id_type=MESH)
-
-    loop(0, others, greet)
+    pl.semaphore_wait(barrier, len(near))
+    for offset in in_column:
+        greet(row_sem, offset)
 
     def iota(shape, dim):
         return lax.broadcasted_iota(jnp.int32, shape, dim)
@@ -124,12 +127,12 @@
         own(k).wait()
 
     pack(0)
-    pl.semaphore_wait(barrier, others)
+    pl.semaphore_wait(row_sem, len(in_column))
     start(0, copy_in, own_in)
 
     def pack_body(k):
         pack(k)
-        start(k, copy_in, own_in)
+        pl.when(k < CHUNKS - 1)(lambda: start(k, copy_in, own_in))
 
     loop(1, CHUNKS, pack_body)
 
@@ -252,6 +255,7 @@
 
     def chunk(k):
         wait(k, copy_in, own_in)
+        pl.when(k == 0)(lambda: start(CHUNKS - 1, copy_in, own_in))
         for r in range(half):
             block = recv_in[k, :, :, r * width0:(r + 1) * width0].astype(F32).reshape(both, width0)
             res = jnp.dot(block.T.astype(BF16), pair, preferred_element_type=F32).astype(BF16)
@@ -320,7 +324,7 @@
             pltpu.VMEM((h2 + 1, (w2 + 1) * c2, lanes), BF16),
             pltpu.VMEM((h3 + 2, (w3 + 2) * c3, lanes), BF16),
             pltpu.VMEM((2, c3, lanes), F32),
-            dma((CHUNKS,)), dma((12,)),
+            pltpu.SemaphoreType.REGULAR, dma((CHUNKS,)), dma((12,)),
             dma((CHUNKS, tiles - 1)), dma((CHUNKS, tiles - 1)), dma((CHUNKS,)),
             dma((CHUNKS, tiles - 1)), dma((CHUNKS, tiles - 1)), dma((CHUNKS,)),
         ],

time: 95.7 us -> 92.4 us (0.966)
  Pallas kernels: 93.7 us -> 90.4 us
    pallas_call x1, Pallas kernels: 93.7 us -> 90.4 us  [encode(): pl.pallas_call(functools.partial(encoder_kernel, cfg), out_shape=jax.Shap...]
where the time goes in v5:
time: 92.4 us; the launch traced here: 92.3 us
  Pallas kernels  90.4 us (98%)
  local copies, waits for them, and re-layouts  1.94 us (2%)
    pallas_call x1, Pallas kernels, encode(): pl.pallas_call(functools.partial(encoder_kernel, cfg), out_shape=jax.Shap...  90.4 us
    transpose x1, local copies, waits for them, and re-layouts, local_forward(): res.transpose(0, 1, 4, 3, 2, 5).reshape(count, th // 8, tw // 8, widths[2])  1.94 us

profile of v5, /device:TPU:97, one launch (start us, length us, event | category | flops | bytes accessed | tf_op | source)
XLA Modules:
  0.0 92.3 jit_solution(1200682668457714403)
XLA Ops:
  0.0 90.4 %shard_map.127 = bf16[4,32,8,8,128]{4,3,2,1,0:T(8,128)(2,1)S(1)} custom-call(bf16[16,64,4,512]{3,2,1,0:T(4,128)(2,1)} %bitcast.6, bf16[3,3,4,32]{3,2,1,0:T(4,128)(2,1)} %refs_0_.1, bf16[3,3,32,32]{3,2,1,0:T(8,128)(2,1)} %refs_1_.1, bf16[3,3,32,64]{3,2,1,0:T(8,128)(2,1)} %refs_2_.1, bf16[3,3,64,64]{3,2,1,0:T(8,128)(2,1)} %refs_3_.1, ...), custom_call_target="tpu_custom_call" | custom-call | tf_op jit(solution)/shard_map/pallas_call | solution.py:306
  90.4 1.9 %copy.14 = bf16[4,32,4,2,8,128]{5,4,3,2,1,0:T(8,128)(2,1)} copy(bf16[4,32,4,2,8,128]{5,2,3,4,1,0:T(4,128)(2,1)S(1)} %bitcast.5) | data formatting | bytes 4194304 | tf_op jit(solution)/shard_map/transpose | solution.py:349

commit v6 on v5

--- a/solution.py
+++ b/solution.py
@@ -12,14 +12,15 @@
 NORM_EPS = 1e-5
 CHUNKS = 4
 SEED = 12
+OUT_SEED = 3
 BLOCKS = ((2, 1, 8), (1, 2, 4), (2, 1, 2), (1, 2, 2), (2, 1, 2), (1, 1, 2))
 MESH = pl.DeviceIdType.MESH
 BF16, F32 = jnp.bfloat16, jnp.float32
 
 
-def send_order(grid_w, grid_h):
+def send_order(grid_w, grid_h, seed=SEED):
     order = list(range(1, grid_w * grid_h))
-    random.Random(SEED).shuffle(order)
+    random.Random(seed).shuffle(order)
     return order
 
 
@@ -117,8 +118,8 @@
     def own_out(k):
         return pltpu.make_async_copy(send_out.at[k, me], out_ref.at[k, me], out_own.at[k])
 
-    def start(k, copy, own):
-        for offset in send_order(grid_w, grid_h):
+    def start(k, copy, own, seed=SEED):
+        for offset in send_order(grid_w, grid_h, seed):
             copy(k, offset - 1).start()
         own(k).start()
 
@@ -286,7 +287,7 @@
             cat = jnp.concatenate([finish(p), finish(p + h * w // 2)], axis=1)
             res = lax.dot_general(pair, cat, (((1,), (1,)), ((), ())), preferred_element_type=F32)
             send_out[k, :, p] = res.reshape(tiles, 2 * imgs, ci).astype(BF16)
-        start(k, copy_out, own_out)
+        start(k, copy_out, own_out, OUT_SEED)
 
     loop(0, CHUNKS, chunk)
     loop(0, CHUNKS, lambda k: wait(k, copy_out, own_out))

time: 92.4 us -> 92.1 us (level)
  no operation moved by 1% of the time
where the time goes in v6:
time: 92.1 us; the launch traced here: 92 us
  Pallas kernels  90 us (98%)
  local copies, waits for them, and re-layouts  1.94 us (2%)
    pallas_call x1, Pallas kernels, encode(): pl.pallas_call(functools.partial(encoder_kernel, cfg), out_shape=jax.Shap...  90 us
    transpose x1, local copies, waits for them, and re-layouts, local_forward(): res.transpose(0, 1, 4, 3, 2, 5).reshape(count, th // 8, tw // 8, widths[2])  1.94 us

profile of v6, /device:TPU:97, one launch (start us, length us, event | category | flops | bytes accessed | tf_op | source)
XLA Modules:
  0.0 92.0 jit_solution(8093346636555359118)
XLA Ops:
  0.0 90.0 %shard_map.127 = bf16[4,32,8,8,128]{4,3,2,1,0:T(8,128)(2,1)S(1)} custom-call(bf16[16,64,4,512]{3,2,1,0:T(4,128)(2,1)} %bitcast.6, bf16[3,3,4,32]{3,2,1,0:T(4,128)(2,1)} %refs_0_.1, bf16[3,3,32,32]{3,2,1,0:T(8,128)(2,1)} %refs_1_.1, bf16[3,3,32,64]{3,2,1,0:T(8,128)(2,1)} %refs_2_.1, bf16[3,3,64,64]{3,2,1,0:T(8,128)(2,1)} %refs_3_.1, ...), custom_call_target="tpu_custom_call" | custom-call | tf_op jit(solution)/shard_map/pallas_call | solution.py:307
  90.0 1.9 %copy.14 = bf16[4,32,4,2,8,128]{5,4,3,2,1,0:T(8,128)(2,1)} copy(bf16[4,32,4,2,8,128]{5,2,3,4,1,0:T(4,128)(2,1)S(1)} %bitcast.5) | data formatting | bytes 4194304 | tf_op jit(solution)/shard_map/transpose | solution.py:350

commit v7 on v6

--- a/solution.py
+++ b/solution.py
@@ -11,7 +11,7 @@
 NORM_GROUPS = 8
 NORM_EPS = 1e-5
 CHUNKS = 4
-SEED = 12
+SEED = 22
 OUT_SEED = 3
 BLOCKS = ((2, 1, 8), (1, 2, 4), (2, 1, 2), (1, 2, 2), (2, 1, 2), (1, 1, 2))
 MESH = pl.DeviceIdType.MESH

time: 92.1 us -> 91.4 us (level)
    pallas_call x1, Pallas kernels: 90 us -> 89.1 us  [encode(): pl.pallas_call(functools.partial(encoder_kernel, cfg), out_shape=jax.Shap...]
where the time goes in v7:
time: 91.4 us; the launch traced here: 91 us
  Pallas kernels  89.1 us (97%)
  local copies, waits for them, and re-layouts  1.94 us (2%)
    pallas_call x1, Pallas kernels, encode(): pl.pallas_call(functools.partial(encoder_kernel, cfg), out_shape=jax.Shap...  89.1 us
    transpose x1, local copies, waits for them, and re-layouts, local_forward(): res.transpose(0, 1, 4, 3, 2, 5).reshape(count, th // 8, tw // 8, widths[2])  1.94 us

profile of v7, /device:TPU:97, one launch (start us, length us, event | category | flops | bytes accessed | tf_op | source)
XLA Modules:
  0.0 91.0 jit_solution(1187320810163455799)
XLA Ops:
  0.0 89.1 %shard_map.127 = bf16[4,32,8,8,128]{4,3,2,1,0:T(8,128)(2,1)S(1)} custom-call(bf16[16,64,4,512]{3,2,1,0:T(4,128)(2,1)} %bitcast.6, bf16[3,3,4,32]{3,2,1,0:T(4,128)(2,1)} %refs_0_.1, bf16[3,3,32,32]{3,2,1,0:T(8,128)(2,1)} %refs_1_.1, bf16[3,3,32,64]{3,2,1,0:T(8,128)(2,1)} %refs_2_.1, bf16[3,3,64,64]{3,2,1,0:T(8,128)(2,1)} %refs_3_.1, ...), custom_call_target="tpu_custom_call" | custom-call | tf_op jit(solution)/shard_map/pallas_call | solution.py:307
  89.1 1.9 %copy.14 = bf16[4,32,4,2,8,128]{5,4,3,2,1,0:T(8,128)(2,1)} copy(bf16[4,32,4,2,8,128]{5,2,3,4,1,0:T(4,128)(2,1)S(1)} %bitcast.5) | data formatting | bytes 4194304 | tf_op jit(solution)/shard_map/transpose | solution.py:350
